TPU v7x, 32 devices: a whole 2x2x4 slice. The times are simulated.
32 devices in a mesh: span: 8 (over z, y), depth: 4 (over x, core).
Axes of the slice: x: 2, y: 2, z: 4, core: 2. Of those that a mesh axis runs over, the one named last changes fastest.
Arguments:
- part_slab: int32 [4, 65536, 1], P('depth', 'span'), may hold values from 0 to 7; in each aligned block of 8192 rows (0 to 8191, 8192 to 16383, ..., all dimensions but the last counted through in order) at most 2048 rows name the same one
- part_cell: int32 [4, 65536], P('depth', 'span'), may hold values from 0 to 65535
- part_volume: float32 [4, 65536], P('depth', 'span'), may hold values from 0.05 to 0.6
- part_drag: float32 [3, 4, 65536], P(None, 'depth', 'span'), may hold values from -6 to 6
- part_count: int32 [4, 8], P('depth', 'span'), may hold values from 7168 to 8192
- prior_solid: float32 [8, 128, 2048], P(None, 'span', 'depth'), may hold values from 0 to 0.6
- prior_drag: float32 [3, 8, 128, 2048], P(None, None, 'span', 'depth'), may hold values from -4 to 4
Outputs:
- fields: float32 [4, 8, 128, 2048], P(None, None, 'span', 'depth')
- feedback: float32 [4, 4, 65536], P(None, 'depth', 'span')
Inputs may be any that keep to these rules, and one draw needn't show every extreme that they name: `part_slab`: among the 8192 particle slots of one owner device, live or not, no slab is named more than 2048 times; in every draw some device names a slab exactly 2048 times.
All inputs are finite; a program needn't handle non-finite values.
Results may differ from a plain program's by a relative error of at most 0.0003.
Values sent between devices are 32-bit elements; how exact they have to be, the bound alone decides.
A program may use at most 128 MiB of HBM per device.

v0:
```python
import functools
import math

import jax
import jax.numpy as jnp
from jax import lax
from jax.experimental import pallas as pl
from jax.experimental.pallas import tpu as pltpu
from jax.sharding import PartitionSpec as P

SWEEPS = 6
NU_WEIGHT = 1.0
PHI_LIMIT = 0.6
BF = jnp.bfloat16
F32 = jnp.float32


def two_parts(value):
    high = value.astype(BF)
    return high, (value - high.astype(F32)).astype(BF)


def hot_of(index, count):
    rows = lax.broadcasted_iota(jnp.int32, (count, index.shape[1]), 0)
    return jnp.where(rows == index, 1.0, 0.0).astype(BF)


def nt_dot(left, right):
    return lax.dot_general(left, right, (((1,), (1,)), ((), ())), preferred_element_type=F32)


def spread(values, row, col, rows, cols):
    mask = lax.broadcasted_iota(jnp.int32, (rows, row.shape[1]), 0) == row
    hot = hot_of(col, cols)
    total = None
    for part in range(2):
        left = jnp.concatenate(
            [jnp.where(mask, two_parts(v)[part].astype(F32), 0.0).astype(BF) for v in values], axis=0
        )
        term = nt_dot(left, hot)
        total = term if total is None else total + term
    return total


def pick(high, low, row, col, rows, cols):
    hot = hot_of(col, cols)
    wide = jnp.dot(high, hot, preferred_element_type=F32)
    wide = wide + jnp.dot(low, hot, preferred_element_type=F32)
    mask = lax.broadcasted_iota(jnp.int32, (rows, row.shape[1]), 0) == row
    comps = high.shape[0] // rows
    found = [
        jnp.sum(jnp.where(mask, wide[c * rows : (c + 1) * rows], 0.0), axis=0, keepdims=True)
        for c in range(comps)
    ]
    return found


def pack_kernel(span, cap, block, count, slab, cell, volume, drag, out, slots):
    rows, cols = out.shape[1:]
    part_rows = slab.shape[1]
    out[...] = jnp.zeros_like(out)
    before_lane = lax.broadcasted_iota(jnp.int32, (block, block), 0)
    this_lane = lax.broadcasted_iota(jnp.int32, (block, block), 1)
    tri = jnp.where(before_lane < this_lane, 1.0, 0.0).astype(BF)
    live_count = count[0, 0]

    def step(b, offset):
        lanes = pl.ds(pl.multiple_of(b * block, block), block)
        sl = slab[:, lanes]
        live = b * block + lax.broadcasted_iota(jnp.int32, (1, block), 1) < live_count
        key = jnp.where(live, sl, -1)
        member = jnp.where(lax.broadcasted_iota(jnp.int32, (span, block), 0) == key, 1.0, 0.0)
        before = jnp.dot(member.astype(BF), tri, preferred_element_type=F32)
        place = jnp.sum(member * (before + offset), axis=0, keepdims=True).astype(jnp.int32)
        slot = jnp.where(live, sl * cap + place, -1)
        slots[:, lanes] = slot
        row = lax.shift_right_arithmetic(slot, int(math.log2(cols)))
        col = lax.bitwise_and(slot, cols - 1)
        values = [cell[:, lanes].astype(F32), volume[:, lanes]]
        values += [drag[c, :, lanes] for c in range(drag.shape[0])]
        out[...] += spread(values, row, col, rows, cols).reshape(out.shape)
        return offset + jnp.sum(member, axis=1, keepdims=True)

    lax.fori_loop(0, part_rows // block, step, jnp.zeros((span, 1), F32))


def x_major(ids, layers, width_x, cols):
    line = lax.shift_right_arithmetic(ids, int(math.log2(cols)))
    layer = lax.shift_right_arithmetic(line, int(math.log2(width_x)))
    return lax.bitwise_and(line, width_x - 1) * layers + layer


def deposit_kernel(group, layers, recv, out):
    comps, rows, cols = out.shape
    out[...] = jnp.zeros_like(out)

    def step(g, carry):
        lines = pl.ds(pl.multiple_of(g * group, group), group)
        block = [recv[c, lines, :] for c in range(comps + 1)]
        flat = [
            jnp.concatenate([b[j : j + 1] for j in range(group)], axis=1) for b in block
        ]
        ids = flat[0].astype(jnp.int32)
        row = x_major(ids, layers, rows // layers, cols)
        col = lax.bitwise_and(ids, cols - 1)
        out[...] += spread(flat[1:], row, col, rows, cols).reshape(out.shape)
        return carry

    lax.fori_loop(0, recv.shape[1] // group, step, 0)
    out[0] = jnp.minimum(out[0], PHI_LIMIT)


def gather_kernel(group, smooth, ids_ref, fields, out, high, low):
    comps, width_x, layers, cols = smooth.shape
    rows = width_x * layers
    for x in range(width_x):
        void = 1.0 - smooth[0, x]
        for c in range(comps):
            value = void if c == 0 else -smooth[c, x] / void
            fields[c, :, x, :] = value
            lines = pl.ds(c * rows + x * layers, layers)
            high[lines], low[lines] = two_parts(value)

    def step(g, carry):
        lines = pl.ds(pl.multiple_of(g * group, group), group)
        block = ids_ref[0, lines, :].astype(jnp.int32)
        found = []
        for j in range(group):
            ids = block[j : j + 1]
            row = x_major(ids, layers, width_x, cols)
            col = lax.bitwise_and(ids, cols - 1)
            found.append(pick(high[...], low[...], row, col, rows, cols))
        for c in range(comps):
            out[c, lines, :] = jnp.concatenate([f[c] for f in found], axis=0)
        return carry

    lax.fori_loop(0, ids_ref.shape[1] // group, step, 0)


def unpack_kernel(block, table_ref, slots, out):
    comps, rows, cols = table_ref.shape
    high, low = two_parts(table_ref[...].reshape(comps * rows, cols))

    def step(b, carry):
        lanes = pl.ds(pl.multiple_of(b * block, block), block)
        slot = slots[:, lanes]
        row = lax.shift_right_arithmetic(slot, int(math.log2(cols)))
        col = lax.bitwise_and(slot, cols - 1)
        found = pick(high, low, row, col, rows, cols)
        for c in range(comps):
            out[c, :, lanes] = found[c]
        return carry

    lax.fori_loop(0, slots.shape[1] // block, step, 0)


MESH = pl.DeviceIdType.MESH
NEAR = [(dx, dy) for dx in (-1, 0, 1) for dy in (-1, 0, 1) if (dx, dy) != (0, 0)]


def exchange_kernel(count, data, out, send_sem, recv_sem, own_sem):
    span, depth = lax.axis_index("span"), lax.axis_index("depth")
    barrier = pltpu.get_barrier_semaphore()
    for k in range(1, count):
        to = lax.rem(span + k, count)
        pl.semaphore_signal(barrier, inc=1, device_id=(to, depth), device_id_type=MESH)
    own = pltpu.make_async_copy(data.at[:, span], out.at[:, span], own_sem)
    own.start()
    pl.semaphore_wait(barrier, count - 1)
    copies = []
    for k in range(1, count):
        to = lax.rem(span + k, count)
        copies.append(
            pltpu.make_async_remote_copy(
                src_ref=data.at[:, to],
                dst_ref=out.at[:, span],
                send_sem=send_sem.at[k],
                recv_sem=recv_sem.at[k],
                device_id=(to, depth),
                device_id_type=MESH,
            )
        )
        copies[-1].start()
    own.wait()
    for copy in copies:
        copy.wait()


def exchange(data, number):
    count = data.shape[1]
    return pl.pallas_call(
        functools.partial(exchange_kernel, count),
        out_shape=jax.ShapeDtypeStruct(data.shape, F32),
        in_specs=[VMEM],
        out_specs=VMEM,
        scratch_shapes=[
            pltpu.SemaphoreType.DMA((count,)),
            pltpu.SemaphoreType.DMA((count,)),
            pltpu.SemaphoreType.DMA,
        ],
        compiler_params=pltpu.CompilerParams(
            vmem_limit_bytes=16 * 1024 * 1024, collective_id=number, has_side_effects=True
        ),
        name=f"exchange_{number}",
    )(data)


def sweeps_kernel(
    rim, solid, drag, above, below, target, out, smooth, source, ysend, yrecv, send_sem, recv_sem
):
    comps, width_x, layers, width_y = target.shape
    span, depth = lax.axis_index("span"), lax.axis_index("depth")
    span_size, depth_size = lax.axis_size("span"), lax.axis_size("depth")
    own = pl.ds(128, width_y)
    total_x = width_x + 2 * rim

    def has(dx, dy):
        x, y = span + dx, depth + dy
        return (x >= 0) & (x < span_size) & (y >= 0) & (y < depth_size)

    barrier = pltpu.get_barrier_semaphore()
    for dx, dy in NEAR:

        @pl.when(has(dx, dy))
        def _(dx=dx, dy=dy):
            pl.semaphore_signal(
                barrier, inc=1, device_id=(span + dx, depth + dy), device_id_type=MESH
            )

    buffers = (smooth, source)

    def copy_of(c, which, at):
        dx, dy = NEAR[at]
        width = rim - which
        buffer = buffers[which]
        if dy == 0 and dx == 1:
            src = buffer.at[c, pl.ds(width_x + rim - width, width), :, own]
            dst = buffer.at[c, pl.ds(rim - width, width), :, own]
        elif dy == 0:
            src = buffer.at[c, pl.ds(rim, width), :, own]
            dst = buffer.at[c, pl.ds(width_x + rim, width), :, own]
        else:
            side = (dy + 1) // 2
            src = ysend.at[which, side, c]
            dst = yrecv.at[which, side, dx + 1, c]
        return pltpu.make_async_remote_copy(
            src_ref=src,
            dst_ref=dst,
            send_sem=send_sem.at[c, which, at],
            recv_sem=recv_sem.at[c, which, at],
            device_id=(span + dx, depth + dy),
            device_id_type=MESH,
        )

    def sides(which):
        return [(at, d) for at, d in enumerate(NEAR) if which == 1 or d[1] != 0]

    def fill_own(c, which, row_of):
        buffer = buffers[which]
        for x in range(width_x):
            buffer[c, rim + x, :, own] = row_of(x)
        for side, start in ((0, 128), (1, width_y)):
            edge = buffer[c, pl.ds(rim, width_x), :, pl.ds(start, 128)]
            turned = edge.reshape(width_x * layers, 128).T
            ysend[which, side, c] = turned[:8] if side == 0 else turned[120:]

    for c in range(comps):
        fill_own(c, 1, lambda x: target[c, x])
        fill_own(c, 0, lambda x: solid[:, x, :] if c == 0 else drag[c - 1, :, x, :])
    count = sum(has(dx, dy).astype(jnp.int32) for dx, dy in NEAR)
    pl.semaphore_wait(barrier, count)
    for c in range(comps):
        for which in range(2):
            for at, (dx, dy) in sides(which):

                @pl.when(has(dx, dy))
                def _(c=c, at=at, which=which):
                    copy_of(c, which, at).start()

    for c in range(comps):
        for r in range(rim):
            smooth[c, r, :, own] = above[c, :, r, :]
            smooth[c, width_x + rim + r, :, own] = below[c, :, r, :]
    for dx, start in ((1, 0), (-1, width_x + rim)):

        @pl.when(jnp.logical_not(has(-dx, 0)))
        def _(start=start):
            source[:, pl.ds(start, rim), :, own] = jnp.zeros((comps, rim, layers, width_y), F32)

    def pads(c, which):
        buffer = buffers[which]
        for at, (dx, dy) in sides(which):
            if dy == 0:

                @pl.when(has(-dx, 0))
                def _(at=at):
                    copy_of(c, which, at).wait_recv()

                continue
            side = (dy + 1) // 2
            lanes = pl.ds(128 + width_y, 128) if side == 0 else pl.ds(0, 128)
            if dx == 0:
                rows, taken = pl.ds(rim, width_x), slice(0, width_x)
            elif dx == 1:
                rows, taken = pl.ds(0, rim), slice(width_x - rim, width_x)
            else:
                rows, taken = pl.ds(width_x + rim, rim), slice(0, rim)

            @pl.when(has(-dx, -dy))
            def _(at=at, side=side, lanes=lanes, rows=rows, taken=taken, dx=dx):
                copy_of(c, which, at).wait_recv()
                block = yrecv[which, side, dx + 1, c]
                rest = jnp.zeros((120, 128), F32)
                parts = [block, rest] if side == 0 else [rest, block]
                turned = jnp.concatenate(parts, axis=0).T.reshape(width_x, layers, 128)
                buffer[c, rows, :, lanes] = turned[taken]

            @pl.when(jnp.logical_not(has(-dx, -dy)))
            def _(lanes=lanes, rows=rows, taken=taken):
                n = taken.stop - taken.start
                buffer[c, rows, :, lanes] = jnp.zeros((n, layers, 128), F32)

    def sent(c, which):
        for at, (dx, dy) in sides(which):

            @pl.when(has(dx, dy))
            def _(at=at):
                copy_of(c, which, at).wait_send()

    lane = lax.broadcasted_iota(jnp.int32, (layers, width_y + 256), 1)
    first = jnp.where(depth > 0, 0, 128)
    end = jnp.where(depth < depth_size - 1, width_y + 256, width_y + 128)
    scale = jnp.where((lane >= first) & (lane < end), 1.0 / (1.0 + 4.0 * NU_WEIGHT), 0.0)
    first_row = jnp.where(span > 0, 0, rim)
    end_row = jnp.where(span < span_size - 1, total_x, width_x + rim)
    for c in range(comps):
        pads(c, 0)
        pads(c, 1)
        for sweep in range(1, SWEEPS + 1):

            def row_step(x, before, c=c):
                here = smooth[c, x]
                beside = before + smooth[c, x + 1]
                beside = beside + pltpu.roll(here, 1, 1) + pltpu.roll(here, width_y + 255, 1)
                inside = jnp.where((x >= first_row) & (x < end_row), 1.0, 0.0)
                smooth[c, x] = (source[c, x] + NU_WEIGHT * beside) * (scale * inside)
                return here

            lax.fori_loop(sweep, total_x - sweep, row_step, smooth[c, sweep - 1], unroll=2)
        out[c] = smooth[c, pl.ds(rim, width_x), :, own]
    for c in range(comps):
        sent(c, 0)
        sent(c, 1)


VMEM = pl.BlockSpec(memory_space=pltpu.VMEM)
SMEM = pl.BlockSpec(memory_space=pltpu.SMEM)
LIMIT = pltpu.CompilerParams(vmem_limit_bytes=48 * 1024 * 1024)


def on_device(part_slab, part_cell, part_volume, part_drag, part_count, prior_solid, prior_drag):
    span_size = lax.axis_size("span")
    part_rows = part_cell.shape[1]
    cap = 2 * part_rows // span_size
    layers, width_x, width_y = prior_solid.shape
    cols = min(256, cap)
    lines = span_size * cap // cols
    block = math.gcd(part_rows, 512)
    rim = SWEEPS
    up = [(i, i + 1) for i in range(span_size - 1)]
    down = [(j, i) for i, j in up]
    edge = jnp.concatenate([prior_solid[None, :, -rim:], prior_drag[:, :, -rim:]], axis=0)
    above = lax.ppermute(edge, "span", up)
    edge = jnp.concatenate([prior_solid[None, :, :rim], prior_drag[:, :, :rim]], axis=0)
    below = lax.ppermute(edge, "span", down)
    packed, slots = pl.pallas_call(
        functools.partial(pack_kernel, span_size, cap, block),
        out_shape=(
            jax.ShapeDtypeStruct((5, lines, cols), F32),
            jax.ShapeDtypeStruct((1, part_rows), jnp.int32),
        ),
        in_specs=[SMEM] + [VMEM] * 4,
        out_specs=(VMEM, VMEM),
        compiler_params=LIMIT,
        name="pack",
    )(part_count, part_slab.reshape(1, part_rows), part_cell, part_volume, part_drag)
    per = lines // span_size
    recv = exchange(packed.reshape(5, span_size, per, cols), 1).reshape(5, lines, cols)
    grid_rows = layers * width_x
    target = pl.pallas_call(
        functools.partial(deposit_kernel, 8, layers),
        out_shape=jax.ShapeDtypeStruct((4, grid_rows, width_y), F32),
        in_specs=[VMEM],
        out_specs=VMEM,
        compiler_params=LIMIT,
        name="deposit",
    )(recv)
    target = target.reshape(4, width_x, layers, width_y)
    wide = (4, width_x + 2 * rim, layers, width_y + 256)
    smooth = pl.pallas_call(
        functools.partial(sweeps_kernel, rim),
        out_shape=jax.ShapeDtypeStruct(target.shape, F32),
        in_specs=[VMEM] * 5,
        out_specs=VMEM,
        scratch_shapes=[
            pltpu.VMEM(wide, F32),
            pltpu.VMEM(wide, F32),
            pltpu.VMEM((2, 2, 4, 8, 128), F32),
            pltpu.VMEM((2, 2, 3, 4, 8, 128), F32),
            pltpu.SemaphoreType.DMA((4, 2, 8)),
            pltpu.SemaphoreType.DMA((4, 2, 8)),
        ],
        compiler_params=pltpu.CompilerParams(
            vmem_limit_bytes=48 * 1024 * 1024, collective_id=0, has_side_effects=True
        ),
        name="sweeps",
    )(prior_solid, prior_drag, above, below, target)
    fields, values = pl.pallas_call(
        functools.partial(gather_kernel, 8),
        out_shape=(
            jax.ShapeDtypeStruct((4, layers, width_x, width_y), F32),
            jax.ShapeDtypeStruct((4, lines, cols), F32),
        ),
        in_specs=[VMEM] * 2,
        out_specs=(VMEM, VMEM),
        scratch_shapes=[pltpu.VMEM((4 * grid_rows, width_y), BF)] * 2,
        compiler_params=LIMIT,
        name="gather",
    )(smooth, recv)
    returned = exchange(values.reshape(4, span_size, per, cols), 2).reshape(4, lines, cols)
    feedback = pl.pallas_call(
        functools.partial(unpack_kernel, block),
        out_shape=jax.ShapeDtypeStruct((4, 1, part_rows), F32),
        in_specs=[VMEM] * 2,
        out_specs=VMEM,
        compiler_params=LIMIT,
        name="unpack",
    )(returned, slots)
    return (fields, feedback)


def solution(mesh):
    in_specs = (
        P("depth", "span", None),
        P("depth", "span"),
        P("depth", "span"),
        P(None, "depth", "span"),
        P("depth", "span"),
        P(None, "span", "depth"),
        P(None, None, "span", "depth"),
    )
    out_specs = (P(None, None, "span", "depth"), P(None, "depth", "span"))
    return jax.shard_map(
        on_device, mesh=mesh, in_specs=in_specs, out_specs=out_specs, check_vma=False
    )
```

profile of v0, /device:TPU:1, one launch (start us, length us, event | category | flops | bytes accessed | tf_op | source)
XLA Modules:
  0.0 136.4 jit_solution(6148727810777758917)
XLA Ops:
  0.6 1.0 slice_bitcast_fusion
  1.6 1.2 fusion
  2.8 0.1 pad_maximum_fusion
  2.9 4.0 %collective-permute-start = (f32[4,8,6,512]{3,2,1,0:T(8,128)S(1)}, f32[4,8,6,512]{3,2,1,0:T(8,128)S(1)}, u32[]{:S(2)}, u32[]{:S(2)}) collective-permute-start(f32[4,8,6,512]{3,2,1,0:T(8,128)S(1)} %pad_maximum_fusion), channel_id=1, source_target_pairs={{0,4},{4,8},{8,12},{12,16},{16,20},{20,24},{24,28},{1,5},{5,9},{9,... | collective-permute-start | bytes 1179656 | tf_op jit(solution)/shard_map/ppermute | solution.py:373
  6.9 0.0 copy-start.2
  6.9 0.0 copy-start.3
  6.9 0.0 copy-start.4
  6.9 0.0 copy-start.5
  6.9 0.1 pad_maximum_fusion.1
  7.0 1.3 collective-permute-start.1
  9.0 0.0 copy-done.2
  9.0 0.0 copy-done.3
  9.0 0.0 copy-done.4
  9.0 0.0 copy-done.5
  9.0 9.8 %pack.1 = (f32[5,64,256]{2,1,0:T(8,128)S(1)}, s32[1,8192]{1,0:T(1,128)S(1)}) custom-call(s32[1,1]{1,0:T(1,128)S(6)} %copy.9.count, s32[1,8192]{1,0:T(1,128)S(1)} %bitcast.16, s32[1,8192]{1,0:T(1,128)S(1)} %copy-done.4, f32[1,8192]{1,0:T(1,128)S(1)} %copy-done.5, f32[3,1,8192]{2,1,0:T(1,128)S(1)} %copy-done.2), custom_call_target="tpu_custom_call" | custom-call | tf_op jit(solution)/shard_map/pack/pallas_call | solution.py:376
  18.8 13.6 %exchange_1.1 = f32[5,8,8,256]{3,2,1,0:T(8,128)S(1)} custom-call(f32[5,8,8,256]{3,2,1,0:T(8,128)S(1)} %bitcast.14), custom_call_target="tpu_custom_call" | custom-call | tf_op jit(solution)/shard_map/exchange_1/pallas_call | solution.py:191
  32.4 0.0 copy-start
  32.4 0.0 copy-start.1
  32.4 20.3 %deposit.1 = f32[4,128,512]{2,1,0:T(8,128)S(1)} custom-call(f32[5,64,256]{2,1,0:T(8,128)S(1)} %bitcast.11), custom_call_target="tpu_custom_call" | custom-call | tf_op jit(solution)/shard_map/deposit/pallas_call | solution.py:390
  52.7 0.0 collective-permute-done.above
  52.7 0.0 collective-permute-done.1.below
  52.7 0.0 copy-done
  52.7 0.0 copy-done.1
  52.7 38.2 %sweeps.1.smooth = f32[4,16,8,512]{3,2,1,0:T(8,128)S(1)} custom-call(f32[8,16,512]{2,1,0:T(8,128)S(1)} %copy-done.1, f32[3,8,16,512]{3,2,1,0:T(8,128)S(1)} %copy-done, f32[4,8,6,512]{3,2,1,0:T(8,128)S(1)} %collective-permute-done.above, f32[4,8,6,512]{3,2,1,0:T(8,128)S(1)} %collective-permute-done.1.below, f32[4,16,8,512]{3,2,1,0:T(8,128)S(1)} %bitcast.10), custom_call_target="tpu_custom_call" | custom-call | tf_op jit(solution)/shard_map/sweeps/pallas_call | solution.py:400
  90.9 22.4 %gather.1 = (f32[4,8,16,512]{3,2,1,0:T(8,128)}, f32[4,64,256]{2,1,0:T(8,128)S(1)}) custom-call(f32[4,16,8,512]{3,2,1,0:T(8,128)S(1)} %sweeps.1.smooth, f32[5,64,256]{2,1,0:T(8,128)S(1)} %bitcast.12), custom_call_target="tpu_custom_call" | custom-call | tf_op jit(solution)/shard_map/gather/pallas_call | solution.py:418
  113.3 17.0 %exchange_2.1 = f32[4,8,8,256]{3,2,1,0:T(8,128)S(1)} custom-call(f32[4,8,8,256]{3,2,1,0:T(8,128)S(1)} %bitcast.15), custom_call_target="tpu_custom_call" | custom-call | tf_op jit(solution)/shard_map/exchange_2/pallas_call | solution.py:191
  130.3 6.1 %unpack.1 = f32[4,1,8192]{2,1,0:T(1,128)} custom-call(f32[4,64,256]{2,1,0:T(8,128)S(1)} %bitcast.13, s32[1,8192]{1,0:T(1,128)S(1)} %get-tuple-element.9.slots), custom_call_target="tpu_custom_call" | custom-call | tf_op jit(solution)/shard_map/unpack/pallas_call | solution.py:431
Async XLA Ops:
  2.9 49.8 %collective-permute-start = (f32[4,8,6,512]{3,2,1,0:T(8,128)S(1)}, f32[4,8,6,512]{3,2,1,0:T(8,128)S(1)}, u32[]{:S(2)}, u32[]{:S(2)}) collective-permute-start(f32[4,8,6,512]{3,2,1,0:T(8,128)S(1)} %pad_maximum_fusion), channel_id=1, source_target_pairs={{0,4},{4,8},{8,12},{12,16},{16,20},{20,24},{24,28},{1,5},{5,9},{9,... | collective-permute-start | bytes 1179656 | tf_op jit(solution)/shard_map/ppermute | solution.py:373
  6.9 2.1 %copy-start.2 = (f32[3,1,8192]{2,1,0:T(1,128)S(1)}, f32[3,1,8192]{2,1,0:T(1,128)}, u32[]{:S(2)}) copy-start(f32[3,1,8192]{2,1,0:T(1,128)} %drag.2) | copy-start | bytes 294916
  6.9 2.1 %copy-start.3 = (s32[1,8192,1]{1,2,0:T(1,128)S(1)}, s32[1,8192,1]{1,2,0:T(1,128)}, u32[]{:S(2)}) copy-start(s32[1,8192,1]{1,2,0:T(1,128)} %param.7) | copy-start | bytes 98308
  6.9 2.1 %copy-start.4 = (s32[1,8192]{1,0:T(1,128)S(1)}, s32[1,8192]{1,0:T(1,128)}, u32[]{:S(2)}) copy-start(s32[1,8192]{1,0:T(1,128)} %cell.1) | copy-start | bytes 98308
  6.9 2.1 %copy-start.5 = (f32[1,8192]{1,0:T(1,128)S(1)}, f32[1,8192]{1,0:T(1,128)}, u32[]{:S(2)}) copy-start(f32[1,8192]{1,0:T(1,128)} %volume.1) | copy-start | bytes 98308
  7.0 45.7 %collective-permute-start.1 = (f32[4,8,6,512]{3,2,1,0:T(8,128)S(1)}, f32[4,8,6,512]{3,2,1,0:T(8,128)S(1)}, u32[]{:S(2)}, u32[]{:S(2)}) collective-permute-start(f32[4,8,6,512]{3,2,1,0:T(8,128)S(1)} %pad_maximum_fusion.1), channel_id=1, source_target_pairs={{4,0},{8,4},{12,8},{16,12},{20,16},{24,20},{28,24},{5,1},{9,5},{13... | collective-permute-start | bytes 1179656 | tf_op jit(solution)/shard_map/ppermute | solution.py:375
  32.4 20.3 %copy-start = (f32[3,8,16,512]{3,2,1,0:T(8,128)S(1)}, f32[3,8,16,512]{3,2,1,0:T(8,128)}, u32[]{:S(2)}) copy-start(f32[3,8,16,512]{3,2,1,0:T(8,128)} %drag.3) | copy-start | bytes 2359300
  32.4 20.3 %copy-start.1 = (f32[8,16,512]{2,1,0:T(8,128)S(1)}, f32[8,16,512]{2,1,0:T(8,128)}, u32[]{:S(2)}) copy-start(f32[8,16,512]{2,1,0:T(8,128)} %solid.1) | copy-start | bytes 786436
where the time goes:
time: 137 us; the launch traced here: 136 us
  Pallas kernels  127 us (93%)
  starting transfers between devices  5.29 us (4%)
  local copies, waits for them, and re-layouts  2.23 us (2%)
  between operations  1.47 us (1%)
    pallas_call x1, Pallas kernels, on_device(): pl.pallas_call(functools.partial(sweeps_kernel, rim), out_shape=jax.Shape...  38.2 us
    pallas_call x2, Pallas kernels, exchange(): pl.pallas_call(functools.partial(exchange_kernel, count), out_shape=jax.S...  30.6 us
    pallas_call x1, Pallas kernels, on_device(): pl.pallas_call(functools.partial(gather_kernel, 8), out_shape=(jax.ShapeD...  22.4 us
    pallas_call x1, Pallas kernels, on_device(): pl.pallas_call(functools.partial(deposit_kernel, 8, layers), out_shape=ja...  20.3 us
    pallas_call x1, Pallas kernels, on_device(): pl.pallas_call(functools.partial(pack_kernel, span_size, cap, block), out...  9.79 us
    pallas_call x1, Pallas kernels, on_device(): pl.pallas_call(functools.partial(unpack_kernel, block), out_shape=jax.Sha...  6.09 us
    ppermute x1, starting transfers between devices, on_device(): above = lax.ppermute(edge, 'span', up)  3.99 us
  transfers between devices with their start and end apart: 2, of which 0 were waited for; matrix products, arithmetic and copies ran while one was open for 0% of the time, Pallas kernels for 32%

commit v1 on v0

v1 whole, which is shorter than its diff:
```python
import functools
import math

import jax
import jax.numpy as jnp
from jax import lax
from jax.experimental import pallas as pl
from jax.experimental.pallas import tpu as pltpu
from jax.sharding import PartitionSpec as P

SWEEPS = 6
NU_WEIGHT = 1.0
PHI_LIMIT = 0.6
BF = jnp.bfloat16
F32 = jnp.float32


def two_parts(value):
    high = value.astype(BF)
    return high, (value - high.astype(F32)).astype(BF)


def nt_dot(left, right):
    return lax.dot_general(left, right, (((1,), (1,)), ((), ())), preferred_element_type=F32)


def hot_at(index, count):
    rows = lax.broadcasted_iota(jnp.int32, (count, index.shape[1]), 0)
    return jnp.where(rows == index, 1.0, 0.0).astype(BF)


def spread(values, row, col, rows, cols):
    mask = hot_at(row, rows)
    parts = [two_parts(v) for v in values]
    left = jnp.concatenate([mask * p[k] for k in range(2) for p in parts], axis=0)
    both = nt_dot(left, hot_at(col, cols))
    n = len(values) * rows
    return both[:n] + both[n:]


class Bins:
    def __init__(self, layers, width_x, width_y, span, lines, cols):
        self.layers, self.span, self.lines, self.line = layers, span, lines, cols
        self.binned = lines == span * layers
        self.cols = min(256, width_y)
        self.parts = width_y // self.cols
        self.rows = width_x * self.parts
        self.width_x, self.width_y = width_x, width_y
        self.log_y, self.log_cols = int(math.log2(width_y)), int(math.log2(self.cols))
        self.log_x = int(math.log2(width_x))

    def place(self, ids):
        y = lax.bitwise_and(ids, self.width_y - 1)
        x = lax.bitwise_and(lax.shift_right_arithmetic(ids, self.log_y), self.width_x - 1)
        row = lax.shift_right_arithmetic(y, self.log_cols) * self.width_x + x
        return self.layer(ids) * self.rows + row, lax.bitwise_and(y, self.cols - 1)

    def layer(self, ids):
        return lax.shift_right_arithmetic(ids, self.log_x + self.log_y)

    def strays(self, ids, line, lane):
        live = ids >= 0
        if not self.binned:
            return live
        own = lax.rem(line, self.layers)
        layer = self.layer(ids)
        beside = jnp.where(lane < self.line // 2, own - 1, own + 1)
        return live & (layer != own) & (layer != beside)

    def any_stray(self, ref):
        ids = ref[0].astype(jnp.int32) - 1
        line, lane = (lax.broadcasted_iota(jnp.int32, ids.shape, axis) for axis in range(2))
        mask = self.strays(ids, line, lane)
        return jnp.max(jnp.where(mask, 1.0, 0.0)) > 0.0

    def pieces(self, j):
        half = self.line // 2
        return [
            (pl.ds(o * self.layers + j, 1), slice(h * half, (h + 1) * half))
            for h in range(2)
            for o in range(self.span)
        ]

    def flat(self, ref, c, j):
        return jnp.concatenate([ref[c, line, lanes] for line, lanes in self.pieces(j)], axis=1)

    def group(self, ref, c, g):
        block = ref[c, pl.ds(pl.multiple_of(g * 8, 8), 8), :]
        return jnp.concatenate([block[k : k + 1] for k in range(8)], axis=1)

    def stray_group(self, ref, g):
        ids = self.group(ref, 0, g).astype(jnp.int32) - 1
        lane = lax.broadcasted_iota(jnp.int32, ids.shape, 1)
        shift = int(math.log2(self.line))
        line = g * 8 + lax.shift_right_arithmetic(lane, shift)
        return ids, self.strays(ids, line, lax.bitwise_and(lane, self.line - 1))


def deposit_kernel(bins, recv, out):
    comps = out.shape[0]
    rows, cols, width_x = bins.rows, bins.cols, bins.width_x
    out[...] = jnp.zeros_like(out)

    def add(layer, sums):
        for c in range(comps):
            for part in range(bins.parts):
                lanes = slice(part * cols, (part + 1) * cols)
                first = c * rows + part * width_x
                out[c, layer, :, lanes] += sums[first : first + width_x]

    if bins.binned:

        for j in range(bins.layers):
            flat = [bins.flat(recv, c, j) for c in range(comps + 1)]
            ids = flat[0].astype(jnp.int32) - 1
            place, col = bins.place(ids)
            hot = hot_at(col, cols)
            parts = [two_parts(v) for v in flat[1:]]
            n = ids.shape[1] // 2

            def sums(layer, lanes, place=place, parts=parts, hot=hot):
                mask = hot_at(place[:, lanes] - layer * rows, rows)
                left = [mask * p[k][:, lanes] for k in range(2) for p in parts]
                both = nt_dot(jnp.concatenate(left, axis=0), hot[:, lanes])
                return both[: comps * rows] + both[comps * rows :]

            add(j, sums(j, slice(0, 2 * n)))
            if j > 0:
                add(j - 1, sums(j - 1, slice(0, n)))
            if j < bins.layers - 1:
                add(j + 1, sums(j + 1, slice(n, 2 * n)))

    @pl.when(bins.any_stray(recv))
    def _():
        def line_step(g, carry):
            ids, mask = bins.stray_group(recv, g)
            place, col = bins.place(ids)
            values = [jnp.where(mask, bins.group(recv, 1 + c, g), 0.0) for c in range(comps)]

            def layer_step(layer, inner):
                add(layer, spread(values, place - layer * rows, col, rows, cols))
                return inner

            return lax.fori_loop(0, bins.layers, layer_step, carry)

        lax.fori_loop(0, bins.lines // 8, line_step, 0)

    out[0] = jnp.minimum(out[0], PHI_LIMIT)


def gather_kernel(bins, smooth, ids_ref, fields, out, tables):
    comps = smooth.shape[0]
    rows, cols, width_x = bins.rows, bins.cols, bins.width_x

    def table_step(layer, carry):
        void = 1.0 - smooth[0, layer]
        for c in range(comps):
            value = void if c == 0 else -smooth[c, layer] / void
            fields[c, layer] = value
            high, low = two_parts(value)
            for part in range(bins.parts):
                lanes = slice(part * cols, (part + 1) * cols)
                first = c * rows + part * width_x
                tables[layer, pl.ds(first, width_x)] = high[:, lanes]
                tables[layer, pl.ds(comps * rows + first, width_x)] = low[:, lanes]
        return carry

    lax.fori_loop(0, bins.layers, table_step, 0)

    def found(layer, place, hot):
        wide = jnp.dot(tables[layer], hot, preferred_element_type=F32)
        row = lax.broadcasted_iota(jnp.int32, (rows, place.shape[1]), 0)
        here = row == place
        values = []
        for c in range(comps):
            value = wide[c * rows : (c + 1) * rows] + wide[(comps + c) * rows : (comps + c + 1) * rows]
            values.append(jnp.sum(jnp.where(here, value, 0.0), axis=0, keepdims=True))
        return values

    if bins.binned:
        half = bins.line // 2

        for j in range(bins.layers):
            ids = bins.flat(ids_ref, 0, j).astype(jnp.int32) - 1
            place, col = bins.place(ids)
            hot = hot_at(col, cols)
            n = ids.shape[1] // 2
            own = found(j, place - j * rows, hot)
            low, high = max(j - 1, 0), min(j + 1, bins.layers - 1)
            left = found(low, place[:, :n] - (j - 1) * rows, hot[:, :n])
            right = found(high, place[:, n:] - (j + 1) * rows, hot[:, n:])
            for c in range(comps):
                value = own[c] + jnp.concatenate([left[c], right[c]], axis=1)
                for at, (line, lanes) in enumerate(bins.pieces(j)):
                    out[c, line, lanes] = value[:, at * half : (at + 1) * half]
    else:
        out[...] = jnp.zeros_like(out)

    @pl.when(bins.any_stray(ids_ref))
    def _():
        def line_step(g, carry):
            ids, mask = bins.stray_group(ids_ref, g)
            place, col = bins.place(ids)
            place = jnp.where(mask, place, -1)
            hot = hot_at(col, cols)

            def layer_step(layer, total):
                at = jnp.where(place >= 0, place - layer * rows, -1)
                more = found(layer, at, hot)
                return [t + m for t, m in zip(total, more)]

            zero = [jnp.zeros(ids.shape, F32)] * comps
            total = lax.fori_loop(0, bins.layers, layer_step, zero)
            for c in range(comps):
                n = bins.line
                block = [total[c][:, k * n : (k + 1) * n] for k in range(8)]
                out[c, pl.ds(pl.multiple_of(g * 8, 8), 8), :] += jnp.concatenate(block, axis=0)
            return carry

        lax.fori_loop(0, bins.lines // 8, line_step, 0)


MESH = pl.DeviceIdType.MESH
RIM = SWEEPS // 2
LANES = 128


class Grid:
    def __init__(self):
        self.span, self.depth = lax.axis_index("span"), lax.axis_index("depth")
        self.span_size, self.depth_size = lax.axis_size("span"), lax.axis_size("depth")

    def has(self, dx, dy):
        x, y = self.span + dx, self.depth + dy
        return (x >= 0) & (x < self.span_size) & (y >= 0) & (y < self.depth_size)

    def peer(self, dx, dy):
        return (self.span + dx, self.depth + dy)

    def signal(self, barrier, dx, dy):
        @pl.when(self.has(dx, dy))
        def _():
            pl.semaphore_signal(barrier, inc=1, device_id=self.peer(dx, dy), device_id_type=MESH)

    def around(self, steps):
        return sum(self.has(dx, dy).astype(jnp.int32) for dx, dy in steps)


X_STEPS = ((-1, 0), (1, 0))
Y_STEPS = ((0, -1), (0, 1))


class Halo:
    def __init__(self, grid, rows_out, rows_in, edge, columns, send_sem, recv_sem):
        self.grid = grid
        self.rows_out, self.rows_in, self.edge, self.columns = rows_out, rows_in, edge, columns
        self.send_sem, self.recv_sem = send_sem, recv_sem

    def _copy(self, src, dst, at, step):
        return pltpu.make_async_remote_copy(
            src_ref=src,
            dst_ref=dst,
            send_sem=self.send_sem(at),
            recv_sem=self.recv_sem(at),
            device_id=self.grid.peer(*step),
            device_id_type=MESH,
        )

    def rows(self, side):
        return self._copy(self.rows_out(side), self.rows_in(1 - side), side, X_STEPS[side])

    def cols(self, part, side):
        at = 2 + 2 * part + side
        return self._copy(self.edge(part, side), self.columns(part, 1 - side), at, Y_STEPS[side])

    def _when(self, step, action):
        @pl.when(self.grid.has(*step))
        def _():
            action()

    def start(self):
        for side in range(2):
            self._when(X_STEPS[side], lambda: self.rows(side).start())
        for side in range(2):
            self._when(Y_STEPS[side], lambda: self.cols(0, side).start())

    def forward(self):
        for side in range(2):
            self._when(X_STEPS[1 - side], lambda: self.rows(side).wait_recv())
        for part in (1, 2):
            for side in range(2):
                self._when(Y_STEPS[side], lambda: self.cols(part, side).start())

    def arrive(self):
        for part in range(3):
            for side in range(2):
                self._when(Y_STEPS[1 - side], lambda: self.cols(part, side).wait_recv())

    def sent(self):
        for side in range(2):
            self._when(X_STEPS[side], lambda: self.rows(side).wait_send())
        for part in range(3):
            for side in range(2):
                self._when(Y_STEPS[side], lambda: self.cols(part, side).wait_send())


HALO_COPIES = 8


def collect_kernel(
    cap, block, wide, layers, shift, count, slab, cell, volume, drag, solid, prior,
    recv, slots, rows_in, cols_in, packed, rows_out, cols_out,
    halo_send, halo_recv, send_sem, recv_sem, own_sem,
):
    grid = Grid()
    span_size = grid.span_size
    values, _, per, cols = recv.shape
    lines = span_size * per
    part_rows = slab.shape[1]
    width_x, width_y = solid.shape[1:]
    comps = 1 + prior.shape[0]
    total_x = width_x + 2 * RIM

    barrier = pltpu.get_barrier_semaphore()
    for k in range(1, span_size):
        to = lax.rem(grid.span + k, span_size)
        pl.semaphore_signal(barrier, inc=1, device_id=(to, grid.depth), device_id_type=MESH)
    for dx, dy in Y_STEPS:
        grid.signal(barrier, dx, dy)

    for c in range(comps):
        field = solid if c == 0 else prior.at[c - 1]
        for x in range(width_x):
            line = field[:, x, :]
            if x < RIM:
                rows_out[c, 0, x] = line
            if x >= width_x - RIM:
                rows_out[c, 1, x - width_x + RIM] = line
            cols_out[c, 0, x] = line[:, :LANES]
            cols_out[c, 1, x] = line[:, width_y - LANES :]
    for side in range(2):

        @pl.when(jnp.logical_not(grid.has(*X_STEPS[side])))
        def _(side=side):
            rows_in[:, side] = jnp.zeros((comps, RIM, layers, width_y), F32)

        @pl.when(jnp.logical_not(grid.has(*Y_STEPS[side])))
        def _(side=side):
            cols_in[:, side] = jnp.zeros((comps, total_x, layers, LANES), F32)

    def edge(part, side):
        if part == 0:
            return cols_out.at[:, side]
        lanes = pl.ds(0 if side == 0 else width_y - LANES, LANES)
        return rows_in.at[:, part - 1, :, :, lanes]

    def columns(part, side):
        first, number = ((RIM, width_x), (0, RIM), (RIM + width_x, RIM))[part]
        return cols_in.at[:, side, pl.ds(first, number)]

    halo = Halo(
        grid, lambda side: rows_out.at[:, side], lambda side: rows_in.at[:, side], edge, columns,
        lambda at: halo_send.at[at], lambda at: halo_recv.at[at],
    )
    pl.semaphore_wait(barrier, span_size - 1 + grid.around(Y_STEPS))
    halo.start()

    keys = layers * span_size
    before_lane = lax.broadcasted_iota(jnp.int32, (block, block), 0)
    this_lane = lax.broadcasted_iota(jnp.int32, (block, block), 1)
    tri = jnp.where(before_lane < this_lane, 1.0, 0.0).astype(BF)
    live_count = count[0, 0]
    many = wide // block

    def lanes_at(first, size):
        return pl.ds(pl.multiple_of(first, size), size)

    def member_of(first):
        lanes = lanes_at(first, block)
        live = first + lax.broadcasted_iota(jnp.int32, (1, block), 1) < live_count
        layer = lax.shift_right_arithmetic(cell[:, lanes], shift)
        key = jnp.where(live, layer * span_size + slab[:, lanes], -1)
        member = jnp.where(lax.broadcasted_iota(jnp.int32, (keys, block), 0) == key, 1.0, 0.0)
        return member, live

    fold = min(block, LANES)

    def tally(b, total):
        for m in range(many):
            member = member_of(b * wide + m * block)[0]
            for k in range(block // fold):
                total = total + member[:, k * fold : (k + 1) * fold]
        return total

    total = lax.fori_loop(0, part_rows // wide, tally, jnp.zeros((keys, fold), F32))
    total = jnp.sum(total, axis=1, keepdims=True)
    counts = [total[k * span_size : (k + 1) * span_size] for k in range(layers)]
    rest = [None] * layers
    left = jnp.zeros((span_size, 1), F32)
    for k in reversed(range(layers)):
        left = left + counts[k]
        rest[k] = left
    base = lax.broadcasted_iota(jnp.int32, (span_size, 1), 0).astype(F32) * cap
    end = jnp.zeros((span_size, 1), F32)
    starts = []
    for k in range(layers):
        start = jnp.minimum(jnp.maximum(end, float(cap // layers * k)), cap - rest[k])
        starts.append(start + base)
        end = start + counts[k]

    def rank(b, offset):
        for m in range(many):
            first = b * wide + m * block
            member, live = member_of(first)
            before = jnp.dot(member.astype(BF), tri, preferred_element_type=F32)
            place = jnp.sum(member * (before + offset), axis=0, keepdims=True).astype(jnp.int32)
            slots[:, lanes_at(first, block)] = jnp.where(live, place, -1)
            offset = offset + jnp.sum(member, axis=1, keepdims=True)
        return offset

    lax.fori_loop(0, part_rows // wide, rank, jnp.concatenate(starts, axis=0))

    groups = ((0, 2), (2, values - 2))
    copies = []
    for at, (first_value, number) in enumerate(groups):
        mine = pl.ds(first_value, number)

        def place_values(b, carry, first_value=first_value, number=number, mine=mine):
            lanes = lanes_at(b * wide, wide)
            slot = slots[:, lanes]
            row = lax.shift_right_arithmetic(slot, int(math.log2(cols)))
            col = lax.bitwise_and(slot, cols - 1)
            taken = []
            for v in range(first_value, first_value + number):
                if v == 0:
                    taken.append((cell[:, lanes] + 1).astype(F32))
                else:
                    taken.append(volume[:, lanes] if v == 1 else drag[v - 2, :, lanes])
            sums = spread(taken, row, col, lines, cols).reshape(number, span_size, per, cols)
            packed[mine] += sums
            return carry

        packed[mine] = jnp.zeros((number, span_size, per, cols), F32)
        lax.fori_loop(0, part_rows // wide, place_values, 0)
        own = pltpu.make_async_copy(
            packed.at[mine, grid.span], recv.at[mine, grid.span], own_sem.at[at]
        )
        own.start()
        copies.append(own)
        for k in range(1, span_size):
            to = lax.rem(grid.span + k, span_size)
            copies.append(
                pltpu.make_async_remote_copy(
                    src_ref=packed.at[mine, to],
                    dst_ref=recv.at[mine, grid.span],
                    send_sem=send_sem.at[at, k],
                    recv_sem=recv_sem.at[at, k],
                    device_id=(to, grid.depth),
                    device_id_type=MESH,
                )
            )
            copies[-1].start()
        if at == 0:
            halo.forward()
    halo.arrive()
    for copy in copies:
        copy.wait()
    halo.sent()


def sweeps_kernel(
    solid, prior, prior_rows, prior_cols, target, out,
    source, first, second, middle, source_cols, middle_cols, send_sem, recv_sem,
):
    grid = Grid()
    comps, layers, width_x, width_y = target.shape
    total_x = width_x + 2 * RIM
    own = pl.ds(0, width_y)
    rest = pl.ds(width_y, LANES)
    own_rows = pl.ds(RIM, width_x)

    barrier = pltpu.get_barrier_semaphore()
    for dx, dy in X_STEPS + Y_STEPS:
        grid.signal(barrier, dx, dy)

    def halo_of(c, phase):
        buffer, cols_in = (source, source_cols) if phase == 0 else (middle, middle_cols)
        width = RIM - 1 if phase == 0 else RIM

        def rows_out(side):
            return buffer.at[c, pl.ds(RIM if side == 0 else RIM + width_x - width, width), :, own]

        def rows_in(side):
            return buffer.at[c, pl.ds(RIM - width if side == 0 else RIM + width_x, width), :, own]

        def rows_of(part):
            return pl.ds(*((RIM, width_x), (RIM - width, width), (RIM + width_x, width))[part])

        def edge(part, side):
            lanes = pl.ds(0 if side == 0 else width_y - LANES, LANES)
            return buffer.at[c, rows_of(part), :, lanes]

        def columns(part, side):
            return cols_in.at[c, side, rows_of(part)]

        return Halo(
            grid, rows_out, rows_in, edge, columns,
            lambda at: send_sem.at[c, phase, at], lambda at: recv_sem.at[c, phase, at],
        )

    halos = [[halo_of(c, phase) for phase in range(2)] for c in range(comps)]
    lane = lax.broadcasted_iota(jnp.int32, (1, layers, LANES), 2)

    def fill_cols(buffer, c, cols_in):
        buffer[c, :, :, rest] = jnp.where(lane < LANES // 2, cols_in[c, 1], cols_in[c, 0])

    for c in range(comps):
        for x in range(width_x):
            source[c, RIM + x, :, own] = target[c, :, x, :]
        if c == 0:
            pl.semaphore_wait(barrier, grid.around(X_STEPS + Y_STEPS))
        halos[c][0].start()
    for side, at in ((0, 0), (1, RIM + width_x)):

        @pl.when(jnp.logical_not(grid.has(*X_STEPS[side])))
        def _(at=at):
            for buffer in (source, middle):
                zeros = jnp.zeros((comps, RIM, layers, width_y), F32)
                buffer[:, pl.ds(at, RIM), :, own] = zeros

        @pl.when(jnp.logical_not(grid.has(*Y_STEPS[side])))
        def _(side=side):
            for buffer in (source_cols, middle_cols):
                buffer[:, side] = jnp.zeros((comps, total_x, layers, LANES), F32)

    for c in range(comps):
        field = solid if c == 0 else prior.at[c - 1]
        for x in range(width_x):
            first[c, RIM + x, :, own] = field[:, x, :]
        first[c, pl.ds(0, RIM), :, own] = prior_rows[c, 0]
        first[c, pl.ds(RIM + width_x, RIM), :, own] = prior_rows[c, 1]
        fill_cols(first, c, prior_cols)

    lanes = lax.broadcasted_iota(jnp.int32, (layers, width_y + LANES), 1)
    known = lanes < width_y
    known = known | ((lanes < width_y + LANES // 2) & (grid.depth < grid.depth_size - 1))
    known = known | ((lanes >= width_y + LANES // 2) & (grid.depth > 0))
    scale = jnp.where(known, 1.0 / (1.0 + 4.0 * NU_WEIGHT), 0.0)

    def relax(c, x, before, here, after):
        beside = before + after
        beside = beside + pltpu.roll(here, 1, 1) + pltpu.roll(here, width_y + LANES - 1, 1)
        return (source[c, x] + NU_WEIGHT * beside) * scale

    def sweep(c, old, new, gone):
        low, high = gone, total_x - gone
        step = max(k for k in range(1, 9) if (high - low) % k == 0)

        def rows(g, carry):
            before, here = carry
            for k in range(step):
                x = low + g * step + k
                after = old[c, x + 1]
                new[c, x] = relax(c, x, before, here, after)
                before, here = here, after
            return before, here

        lax.fori_loop(0, (high - low) // step, rows, (old[c, low - 1], old[c, low]))
        for side, x in ((0, RIM - 1), (1, RIM + width_x)):
            if low <= x < high:

                @pl.when(jnp.logical_not(grid.has(*X_STEPS[side])))
                def _(x=x):
                    new[c, x] = jnp.zeros((layers, width_y + LANES), F32)

    def first_half(c):
        halos[c][0].arrive()
        fill_cols(source, c, source_cols)
        sweep(c, first, second, 1)
        sweep(c, second, first, 2)
        sweep(c, first, middle, 3)
        halos[c][1].start()

    def second_half(c):
        halos[c][1].arrive()
        fill_cols(middle, c, middle_cols)
        sweep(c, middle, first, 1)
        sweep(c, first, second, 2)
        before, here = second[c, RIM - 1], second[c, RIM]
        for x in range(width_x):
            after = second[c, RIM + x + 1]
            out[c, :, x, :] = relax(c, RIM + x, before, here, after)[:, :width_y]
            before, here = here, after

    halos[0][0].forward()
    for c in range(comps):
        if c + 1 < comps:
            halos[c + 1][0].forward()
        first_half(c)
    halos[0][1].forward()
    for c in range(comps):
        if c + 1 < comps:
            halos[c + 1][1].forward()
        second_half(c)
    for c in range(comps):
        for phase in range(2):
            halos[c][phase].sent()


def feedback_kernel(wide, values, slots, out, table, hots, send_sem, recv_sem, own_sem):
    grid = Grid()
    comps, span_size, per, cols = values.shape
    lines = span_size * per
    part_rows = slots.shape[1]
    barrier = pltpu.get_barrier_semaphore()
    for k in range(1, span_size):
        to = lax.rem(grid.span + k, span_size)
        pl.semaphore_signal(barrier, inc=1, device_id=(to, grid.depth), device_id_type=MESH)
    pl.semaphore_wait(barrier, span_size - 1)
    groups = (pl.ds(0, comps // 2), pl.ds(comps // 2, comps - comps // 2))
    copies = []
    for at, mine in enumerate(groups):
        own = pltpu.make_async_copy(
            values.at[mine, grid.span], table.at[mine, grid.span], own_sem.at[at]
        )
        own.start()
        copies.append([own])
        for k in range(1, span_size):
            to = lax.rem(grid.span + k, span_size)
            copies[at].append(
                pltpu.make_async_remote_copy(
                    src_ref=values.at[mine, to],
                    dst_ref=table.at[mine, grid.span],
                    send_sem=send_sem.at[at, k],
                    recv_sem=recv_sem.at[at, k],
                    device_id=(to, grid.depth),
                    device_id_type=MESH,
                )
            )
            copies[at][-1].start()

    def lanes_at(b):
        return pl.ds(pl.multiple_of(b * wide, wide), wide)

    def hot_step(b, carry):
        lanes = lanes_at(b)
        hots[:, lanes] = hot_at(lax.bitwise_and(slots[:, lanes], cols - 1), cols)
        return carry

    lax.fori_loop(0, part_rows // wide, hot_step, 0)
    for at, mine in enumerate(groups):
        for copy in copies[at]:
            copy.wait()
        number = mine.size
        high, low = two_parts(table[mine].reshape(number * lines, cols))
        both = jnp.concatenate([high, low], axis=0)

        def pick_step(b, carry, mine=mine, number=number, both=both):
            lanes = lanes_at(b)
            row = lax.shift_right_arithmetic(slots[:, lanes], int(math.log2(cols)))
            wanted = lax.broadcasted_iota(jnp.int32, (lines, wide), 0) == row
            found = jnp.dot(both, hots[:, lanes], preferred_element_type=F32)
            for c in range(number):
                value = found[c * lines : (c + 1) * lines]
                value = value + found[(number + c) * lines : (number + c + 1) * lines]
                value = jnp.sum(jnp.where(wanted, value, 0.0), axis=0, keepdims=True)
                out[mine.start + c, :, lanes] = value
            return carry

        lax.fori_loop(0, part_rows // wide, pick_step, 0)


VMEM = pl.BlockSpec(memory_space=pltpu.VMEM)
SMEM = pl.BlockSpec(memory_space=pltpu.SMEM)
LIMIT = pltpu.CompilerParams(vmem_limit_bytes=48 * 1024 * 1024)


def far(number):
    return pltpu.CompilerParams(
        vmem_limit_bytes=48 * 1024 * 1024, collective_id=number, has_side_effects=True
    )


def on_device(part_slab, part_cell, part_volume, part_drag, part_count, prior_solid, prior_drag):
    span_size = lax.axis_size("span")
    part_rows = part_cell.shape[1]
    cap = 2 * part_rows // span_size
    layers, width_x, width_y = prior_solid.shape
    cols = min(256, cap)
    lines = span_size * cap // cols
    per = lines // span_size
    block = math.gcd(part_rows, 512)
    wide = math.gcd(part_rows, 2048)
    total_x = width_x + 2 * RIM
    dma = pltpu.SemaphoreType.DMA
    recv, slots, prior_rows, prior_cols = pl.pallas_call(
        functools.partial(
            collect_kernel, cap, block, wide, layers, int(math.log2(width_x * width_y))
        ),
        out_shape=(
            jax.ShapeDtypeStruct((5, span_size, per, cols), F32),
            jax.ShapeDtypeStruct((1, part_rows), jnp.int32),
            jax.ShapeDtypeStruct((4, 2, RIM, layers, width_y), F32),
            jax.ShapeDtypeStruct((4, 2, total_x, layers, LANES), F32),
        ),
        in_specs=[SMEM] + [VMEM] * 6,
        out_specs=(VMEM,) * 4,
        scratch_shapes=[
            pltpu.VMEM((5, span_size, per, cols), F32),
            pltpu.VMEM((4, 2, RIM, layers, width_y), F32),
            pltpu.VMEM((4, 2, width_x, layers, LANES), F32),
            dma((HALO_COPIES,)),
            dma((HALO_COPIES,)),
            dma((2, span_size)),
            dma((2, span_size)),
            dma((2,)),
        ],
        compiler_params=far(1),
        name="collect",
    )(
        part_count, part_slab.reshape(1, part_rows), part_cell, part_volume, part_drag,
        prior_solid, prior_drag,
    )
    recv = recv.reshape(5, lines, cols)
    bins = Bins(layers, width_x, width_y, span_size, lines, cols)
    target = pl.pallas_call(
        functools.partial(deposit_kernel, bins),
        out_shape=jax.ShapeDtypeStruct((4, layers, width_x, width_y), F32),
        in_specs=[VMEM],
        out_specs=VMEM,
        compiler_params=LIMIT,
        name="deposit",
    )(recv)
    whole = pltpu.VMEM((4, total_x, layers, width_y + LANES), F32)
    columns = pltpu.VMEM((4, 2, total_x, layers, LANES), F32)
    smooth = pl.pallas_call(
        sweeps_kernel,
        out_shape=jax.ShapeDtypeStruct(target.shape, F32),
        in_specs=[VMEM] * 5,
        out_specs=VMEM,
        scratch_shapes=[whole] * 4 + [columns] * 2 + [dma((4, 2, HALO_COPIES))] * 2,
        compiler_params=far(0),
        name="sweeps",
    )(prior_solid, prior_drag, prior_rows, prior_cols, target)
    fields, values = pl.pallas_call(
        functools.partial(gather_kernel, bins),
        out_shape=(
            jax.ShapeDtypeStruct((4, layers, width_x, width_y), F32),
            jax.ShapeDtypeStruct((4, lines, cols), F32),
        ),
        in_specs=[VMEM] * 2,
        out_specs=(VMEM, VMEM),
        scratch_shapes=[pltpu.VMEM((layers, 8 * bins.rows, bins.cols), BF)],
        compiler_params=LIMIT,
        name="gather",
    )(smooth, recv)
    feedback = pl.pallas_call(
        functools.partial(feedback_kernel, wide),
        out_shape=jax.ShapeDtypeStruct((4, 1, part_rows), F32),
        in_specs=[VMEM] * 2,
        out_specs=VMEM,
        scratch_shapes=[
            pltpu.VMEM((4, span_size, per, cols), F32),
            pltpu.VMEM((cols, part_rows), BF),
            dma((2, span_size)),
            dma((2, span_size)),
            dma((2,)),
        ],
        compiler_params=far(2),
        name="feedback",
    )(values.reshape(4, span_size, per, cols), slots)
    return (fields, feedback)


def solution(mesh):
    in_specs = (
        P("depth", "span", None),
        P("depth", "span"),
        P("depth", "span"),
        P(None, "depth", "span"),
        P("depth", "span"),
        P(None, "span", "depth"),
        P(None, None, "span", "depth"),
    )
    out_specs = (P(None, None, "span", "depth"), P(None, "depth", "span"))
    return jax.shard_map(
        on_device, mesh=mesh, in_specs=in_specs, out_specs=out_specs, check_vma=False
    )
```

time: 137 us -> 82.1 us (0.60)
  Pallas kernels: 127 us -> 74.4 us
  starting transfers between devices: 5.29 us -> 0 us
  local copies, waits for them, and re-layouts: 2.23 us -> 5.91 us
    pallas_call x7 -> x5, Pallas kernels: 127 us -> 74.4 us  [the longest x1 25 us: on_device(): pl.pallas_call(sweeps_kernel, out_shape=jax.ShapeDtypeStruct(target.shape...]
    unnamed x12 -> x15, local copies, waits for them, and re-layouts: 0.04 us -> 5.91 us
    ppermute x2 -> x0, starting transfers between devices: 5.29 us -> none  [the longest x1 3.99 us: on_device(): above = lax.ppermute(edge, 'span', up)]
  transfers between devices with their start and end apart: 2 -> 0, of which waited for: 0 -> 0; matrix products, arithmetic and copies ran while one was open for 0% -> 0% of each run, Pallas kernels for 32% -> 0%
where the time goes in v1:
time: 82.1 us; the launch traced here: 81.7 us
  Pallas kernels  74.4 us (91%)
  local copies, waits for them, and re-layouts  5.91 us (7%)
  between operations  1.34 us (2%)
    pallas_call x1, Pallas kernels, on_device(): pl.pallas_call(sweeps_kernel, out_shape=jax.ShapeDtypeStruct(target.shape...  25 us
    pallas_call x1, Pallas kernels, on_device(): pl.pallas_call(functools.partial(collect_kernel, cap, block, wide, layers...  22.5 us
    pallas_call x1, Pallas kernels, on_device(): pl.pallas_call(functools.partial(feedback_kernel, wide), out_shape=jax.Sh...  14 us
    pallas_call x1, Pallas kernels, on_device(): pl.pallas_call(functools.partial(gather_kernel, bins), out_shape=(jax.Sha...  8.25 us
    unnamed x15, local copies, waits for them, and re-layouts  5.91 us
    pallas_call x1, Pallas kernels, on_device(): pl.pallas_call(functools.partial(deposit_kernel, bins), out_shape=jax.Sha...  4.64 us

profile of v1, /device:TPU:1, one launch (start us, length us, event | category | flops | bytes accessed | tf_op | source)
XLA Modules:
  0.0 81.7 jit_solution(2098823415992269188)
XLA Ops:
  1.3 0.0 copy-start
  1.3 1.1 %copy-done = f32[3,8,16,512]{3,2,1,0:T(8,128)S(1)} copy-done((f32[3,8,16,512]{3,2,1,0:T(8,128)S(1)}, f32[3,8,16,512]{3,2,1,0:T(8,128)}, u32[]{:S(2)}) %copy-start) | copy-done | bytes 786456
  2.4 0.0 copy-start.2
  2.4 0.9 %copy-done.2 = f32[8,16,512]{2,1,0:T(8,128)S(1)} copy-done((f32[8,16,512]{2,1,0:T(8,128)S(1)}, f32[8,16,512]{2,1,0:T(8,128)}, u32[]{:S(2)}) %copy-start.2) | copy-done | bytes 262168
  3.4 0.0 copy-start.3
  3.4 0.9 %copy-done.3 = f32[3,1,8192]{2,1,0:T(1,128)S(1)} copy-done((f32[3,1,8192]{2,1,0:T(1,128)S(1)}, f32[3,1,8192]{2,1,0:T(1,128)}, u32[]{:S(2)}) %copy-start.3) | copy-done | bytes 98328
  4.3 0.0 copy-start.4
  4.3 0.8 copy-done.4
  5.0 0.0 copy-start.5
  5.0 0.8 copy-done.5
  5.8 0.0 copy-start.6
  5.8 0.8 copy-done.6
  6.5 22.5 %collect.1 = (f32[5,8,8,256]{3,2,1,0:T(8,128)S(1)}, s32[1,8192]{1,0:T(1,128)S(1)}, f32[4,2,3,8,512]{4,3,2,1,0:T(8,128)S(1)}, f32[4,2,22,8,128]{4,3,2,1,0:T(8,128)S(1)}) custom-call(s32[1,1]{1,0:T(1,128)S(6)} %copy.10.count, s32[1,8192]{1,0:T(1,128)S(1)} %bitcast.6, s32[1,8192]{1,0:T(1,128)S(1)} %copy-done.5, f32[1,8192]{1,0:T(1,128)S(1)} %copy-done.6, ...), custom_call_target="tpu_custom_call" | custom-call | tf_op jit(solution)/shard_map/collect/pallas_call | solution.py:696
  29.1 0.0 copy-start.1
  29.1 4.6 %deposit.1.target = f32[4,8,16,512]{3,2,1,0:T(8,128)S(1)} custom-call(f32[5,64,256]{2,1,0:T(8,128)S(1)} %bitcast.3), custom_call_target="tpu_custom_call" | custom-call | tf_op jit(solution)/shard_map/deposit/pallas_call | solution.py:726
  33.7 0.0 copy-done.1
  33.7 25.0 %sweeps.1.smooth = f32[4,8,16,512]{3,2,1,0:T(8,128)S(1)} custom-call(f32[8,16,512]{2,1,0:T(8,128)S(1)} %copy-done.2, f32[3,8,16,512]{3,2,1,0:T(8,128)S(1)} %copy-done.1, f32[4,2,3,8,512]{4,3,2,1,0:T(8,128)S(1)} %get-tuple-element.8.prior_rows, f32[4,2,22,8,128]{4,3,2,1,0:T(8,128)S(1)} %get-tuple-element.9.prior_cols, f32[4,8,16,512]{3,2,1,0:T(8,128)S(1)} %deposit.1.target), custom_call_target="tpu_custom_call" | custom-call | tf_op jit(solution)/shard_map/sweeps/pallas_call | solution.py:736
  58.8 8.3 %gather.1 = (f32[4,8,16,512]{3,2,1,0:T(8,128)}, f32[4,64,256]{2,1,0:T(8,128)S(1)}) custom-call(f32[4,8,16,512]{3,2,1,0:T(8,128)S(1)} %sweeps.1.smooth, f32[5,64,256]{2,1,0:T(8,128)S(1)} %bitcast.4), custom_call_target="tpu_custom_call" | custom-call | tf_op jit(solution)/shard_map/gather/pallas_call | solution.py:745
  67.0 14.0 %feedback.1 = f32[4,1,8192]{2,1,0:T(1,128)S(1)} custom-call(f32[4,8,8,256]{3,2,1,0:T(8,128)S(1)} %bitcast.5, s32[1,8192]{1,0:T(1,128)S(1)} %get-tuple-element.13.slots), custom_call_target="tpu_custom_call" | custom-call | tf_op jit(solution)/shard_map/feedback/pallas_call | solution.py:757
  81.0 0.7 copy.11
Async XLA Ops:
  1.3 1.1 %copy-start = (f32[3,8,16,512]{3,2,1,0:T(8,128)S(1)}, f32[3,8,16,512]{3,2,1,0:T(8,128)}, u32[]{:S(2)}) copy-start(f32[3,8,16,512]{3,2,1,0:T(8,128)} %prior.3) | copy-start | bytes 2359300
  2.4 0.9 %copy-start.2 = (f32[8,16,512]{2,1,0:T(8,128)S(1)}, f32[8,16,512]{2,1,0:T(8,128)}, u32[]{:S(2)}) copy-start(f32[8,16,512]{2,1,0:T(8,128)} %solid.3) | copy-start | bytes 786436
  3.4 0.9 %copy-start.3 = (f32[3,1,8192]{2,1,0:T(1,128)S(1)}, f32[3,1,8192]{2,1,0:T(1,128)}, u32[]{:S(2)}) copy-start(f32[3,1,8192]{2,1,0:T(1,128)} %drag.1) | copy-start | bytes 294916
  4.3 0.8 copy-start.4
  5.0 0.8 copy-start.5
  5.8 0.8 copy-start.6
  29.1 4.7 %copy-start.1 = (f32[3,8,16,512]{3,2,1,0:T(8,128)S(1)}, f32[3,8,16,512]{3,2,1,0:T(8,128)}, u32[]{:S(2)}) copy-start(f32[3,8,16,512]{3,2,1,0:T(8,128)} %prior.3) | copy-start | bytes 2359300

commit v2 on v1

--- a/solution.py
+++ b/solution.py
@@ -308,10 +308,18 @@
 
 
 def collect_kernel(
-    cap, block, wide, layers, shift, count, slab, cell, volume, drag, solid, prior,
-    recv, slots, rows_in, cols_in, packed, rows_out, cols_out,
-    halo_send, halo_recv, send_sem, recv_sem, own_sem,
+    cap, block, wide, layers, shift, count, slab_far, cell_far, volume_far, drag_far, solid_far,
+    prior_far, recv, slots, rows_in, cols_in, packed, rows_out, cols_out,
+    slab, cell, volume, drag, solid, prior, halo_send, halo_recv, send_sem, recv_sem, own_sem,
+    near_sem,
 ):
+    pairs = (
+        (slab_far, slab), (cell_far, cell), (solid_far, solid), (prior_far, prior),
+        (volume_far, volume), (drag_far, drag),
+    )
+    near = [pltpu.make_async_copy(a, b, near_sem.at[k]) for k, (a, b) in enumerate(pairs)]
+    for copy in near:
+        copy.start()
     grid = Grid()
     span_size = grid.span_size
     values, _, per, cols = recv.shape
@@ -328,6 +336,35 @@
     for dx, dy in Y_STEPS:
         grid.signal(barrier, dx, dy)
 
+    keys = layers * span_size
+    live_count = count[0, 0]
+    many = wide // block
+
+    def lanes_at(first, size):
+        return pl.ds(pl.multiple_of(first, size), size)
+
+    def member_of(first):
+        lanes = lanes_at(first, block)
+        live = first + lax.broadcasted_iota(jnp.int32, (1, block), 1) < live_count
+        layer = lax.shift_right_arithmetic(cell[:, lanes], shift)
+        key = jnp.where(live, layer * span_size + slab[:, lanes], -1)
+        member = jnp.where(lax.broadcasted_iota(jnp.int32, (keys, block), 0) == key, 1.0, 0.0)
+        return member, live
+
+    fold = min(block, LANES)
+
+    def tally(b, total):
+        for m in range(many):
+            member = member_of(b * wide + m * block)[0]
+            for k in range(block // fold):
+                total = total + member[:, k * fold : (k + 1) * fold]
+        return total
+
+    near[0].wait()
+    near[1].wait()
+    total = lax.fori_loop(0, part_rows // wide, tally, jnp.zeros((keys, fold), F32))
+    near[2].wait()
+    near[3].wait()
     for c in range(comps):
         field = solid if c == 0 else prior.at[c - 1]
         for x in range(width_x):
@@ -365,34 +402,9 @@
     pl.semaphore_wait(barrier, span_size - 1 + grid.around(Y_STEPS))
     halo.start()
 
-    keys = layers * span_size
     before_lane = lax.broadcasted_iota(jnp.int32, (block, block), 0)
     this_lane = lax.broadcasted_iota(jnp.int32, (block, block), 1)
     tri = jnp.where(before_lane < this_lane, 1.0, 0.0).astype(BF)
-    live_count = count[0, 0]
-    many = wide // block
-
-    def lanes_at(first, size):
-        return pl.ds(pl.multiple_of(first, size), size)
-
-    def member_of(first):
-        lanes = lanes_at(first, block)
-        live = first + lax.broadcasted_iota(jnp.int32, (1, block), 1) < live_count
-        layer = lax.shift_right_arithmetic(cell[:, lanes], shift)
-        key = jnp.where(live, layer * span_size + slab[:, lanes], -1)
-        member = jnp.where(lax.broadcasted_iota(jnp.int32, (keys, block), 0) == key, 1.0, 0.0)
-        return member, live
-
-    fold = min(block, LANES)
-
-    def tally(b, total):
-        for m in range(many):
-            member = member_of(b * wide + m * block)[0]
-            for k in range(block // fold):
-                total = total + member[:, k * fold : (k + 1) * fold]
-        return total
-
-    total = lax.fori_loop(0, part_rows // wide, tally, jnp.zeros((keys, fold), F32))
     total = jnp.sum(total, axis=1, keepdims=True)
     counts = [total[k * span_size : (k + 1) * span_size] for k in range(layers)]
     rest = [None] * layers
@@ -420,6 +432,8 @@
 
     lax.fori_loop(0, part_rows // wide, rank, jnp.concatenate(starts, axis=0))
 
+    near[4].wait()
+    near[5].wait()
     groups = ((0, 2), (2, values - 2))
     copies = []
     for at, (first_value, number) in enumerate(groups):
@@ -460,8 +474,7 @@
                 )
             )
             copies[-1].start()
-        if at == 0:
-            halo.forward()
+    halo.forward()
     halo.arrive()
     for copy in copies:
         copy.wait()
@@ -517,22 +530,6 @@
     for c in range(comps):
         for x in range(width_x):
             source[c, RIM + x, :, own] = target[c, :, x, :]
-        if c == 0:
-            pl.semaphore_wait(barrier, grid.around(X_STEPS + Y_STEPS))
-        halos[c][0].start()
-    for side, at in ((0, 0), (1, RIM + width_x)):
-
-        @pl.when(jnp.logical_not(grid.has(*X_STEPS[side])))
-        def _(at=at):
-            for buffer in (source, middle):
-                zeros = jnp.zeros((comps, RIM, layers, width_y), F32)
-                buffer[:, pl.ds(at, RIM), :, own] = zeros
-
-        @pl.when(jnp.logical_not(grid.has(*Y_STEPS[side])))
-        def _(side=side):
-            for buffer in (source_cols, middle_cols):
-                buffer[:, side] = jnp.zeros((comps, total_x, layers, LANES), F32)
-
     for c in range(comps):
         field = solid if c == 0 else prior.at[c - 1]
         for x in range(width_x):
@@ -540,6 +537,22 @@
         first[c, pl.ds(0, RIM), :, own] = prior_rows[c, 0]
         first[c, pl.ds(RIM + width_x, RIM), :, own] = prior_rows[c, 1]
         fill_cols(first, c, prior_cols)
+
+    pl.semaphore_wait(barrier, grid.around(X_STEPS + Y_STEPS))
+    for c in range(comps):
+        halos[c][0].start()
+    for side, at in ((0, 0), (1, RIM + width_x)):
+
+        @pl.when(jnp.logical_not(grid.has(*X_STEPS[side])))
+        def _(at=at):
+            for buffer in (source, middle):
+                zeros = jnp.zeros((comps, RIM, layers, width_y), F32)
+                buffer[:, pl.ds(at, RIM), :, own] = zeros
+
+        @pl.when(jnp.logical_not(grid.has(*Y_STEPS[side])))
+        def _(side=side):
+            for buffer in (source_cols, middle_cols):
+                buffer[:, side] = jnp.zeros((comps, total_x, layers, LANES), F32)
 
     lanes = lax.broadcasted_iota(jnp.int32, (layers, width_y + LANES), 1)
     known = lanes < width_y
@@ -616,6 +629,15 @@
     for k in range(1, span_size):
         to = lax.rem(grid.span + k, span_size)
         pl.semaphore_signal(barrier, inc=1, device_id=(to, grid.depth), device_id_type=MESH)
+    def lanes_at(b):
+        return pl.ds(pl.multiple_of(b * wide, wide), wide)
+
+    def hot_step(b, carry):
+        lanes = lanes_at(b)
+        hots[:, lanes] = hot_at(lax.bitwise_and(slots[:, lanes], cols - 1), cols)
+        return carry
+
+    lax.fori_loop(0, part_rows // wide, hot_step, 0)
     pl.semaphore_wait(barrier, span_size - 1)
     groups = (pl.ds(0, comps // 2), pl.ds(comps // 2, comps - comps // 2))
     copies = []
@@ -639,15 +661,6 @@
             )
             copies[at][-1].start()
 
-    def lanes_at(b):
-        return pl.ds(pl.multiple_of(b * wide, wide), wide)
-
-    def hot_step(b, carry):
-        lanes = lanes_at(b)
-        hots[:, lanes] = hot_at(lax.bitwise_and(slots[:, lanes], cols - 1), cols)
-        return carry
-
-    lax.fori_loop(0, part_rows // wide, hot_step, 0)
     for at, mine in enumerate(groups):
         for copy in copies[at]:
             copy.wait()
@@ -672,6 +685,7 @@
 
 VMEM = pl.BlockSpec(memory_space=pltpu.VMEM)
 SMEM = pl.BlockSpec(memory_space=pltpu.SMEM)
+HBM = pl.BlockSpec(memory_space=pltpu.HBM)
 LIMIT = pltpu.CompilerParams(vmem_limit_bytes=48 * 1024 * 1024)
 
 
@@ -703,23 +717,36 @@
             jax.ShapeDtypeStruct((4, 2, RIM, layers, width_y), F32),
             jax.ShapeDtypeStruct((4, 2, total_x, layers, LANES), F32),
         ),
-        in_specs=[SMEM] + [VMEM] * 6,
+        in_specs=[SMEM] + [HBM] * 6,
         out_specs=(VMEM,) * 4,
         scratch_shapes=[
             pltpu.VMEM((5, span_size, per, cols), F32),
             pltpu.VMEM((4, 2, RIM, layers, width_y), F32),
             pltpu.VMEM((4, 2, width_x, layers, LANES), F32),
+            pltpu.VMEM((1, part_rows), jnp.int32),
+            pltpu.VMEM((1, part_rows), jnp.int32),
+            pltpu.VMEM((1, part_rows), F32),
+            pltpu.VMEM(part_drag.shape, F32),
+            pltpu.VMEM(prior_solid.shape, F32),
+            pltpu.VMEM(prior_drag.shape, F32),
             dma((HALO_COPIES,)),
             dma((HALO_COPIES,)),
             dma((2, span_size)),
             dma((2, span_size)),
             dma((2,)),
+            dma((6,)),
         ],
         compiler_params=far(1),
         name="collect",
     )(
-        part_count, part_slab.reshape(1, part_rows), part_cell, part_volume, part_drag,
-        prior_solid, prior_drag,
+        part_count,
+        *[
+            pltpu.with_memory_space_constraint(a, pltpu.HBM)
+            for a in (
+                part_slab.reshape(1, part_rows), part_cell, part_volume, part_drag,
+                prior_solid, prior_drag,
+            )
+        ],
     )
     recv = recv.reshape(5, lines, cols)
     bins = Bins(layers, width_x, width_y, span_size, lines, cols)

time: 82.1 us -> 72.6 us (0.88)
  local copies, waits for them, and re-layouts: 5.91 us -> 0.67 us
  Pallas kernels: 74.4 us -> 70.5 us
    unnamed x15 -> x5, local copies, waits for them, and re-layouts: 5.91 us -> 0.67 us
    pallas_call x1, Pallas kernels: 22.5 us -> 18 us  [on_device(): pl.pallas_call(functools.partial(collect_kernel, cap, block, wide, layers...]
    pallas_call x1, Pallas kernels: 25 us -> 27.9 us  [on_device(): pl.pallas_call(sweeps_kernel, out_shape=jax.ShapeDtypeStruct(target.shape...]
    pallas_call x1, Pallas kernels: 14 us -> 11.7 us  [on_device(): pl.pallas_call(functools.partial(feedback_kernel, wide), out_shape=jax.Sh...]
where the time goes in v2:
time: 72.6 us; the launch traced here: 72.5 us
  Pallas kernels  70.5 us (97%)
  between operations  1.34 us (2%)
    pallas_call x1, Pallas kernels, on_device(): pl.pallas_call(sweeps_kernel, out_shape=jax.ShapeDtypeStruct(target.shape...  27.9 us
    pallas_call x1, Pallas kernels, on_device(): pl.pallas_call(functools.partial(collect_kernel, cap, block, wide, layers...  18 us
    pallas_call x1, Pallas kernels, on_device(): pl.pallas_call(functools.partial(feedback_kernel, wide), out_shape=jax.Sh...  11.7 us
    pallas_call x1, Pallas kernels, on_device(): pl.pallas_call(functools.partial(gather_kernel, bins), out_shape=(jax.Sha...  8.26 us
    pallas_call x1, Pallas kernels, on_device(): pl.pallas_call(functools.partial(deposit_kernel, bins), out_shape=jax.Sha...  4.65 us

profile of v2, /device:TPU:1, one launch (start us, length us, event | category | flops | bytes accessed | tf_op | source)
XLA Modules:
  0.0 72.5 jit_solution(15657503685381664859)
XLA Ops:
  1.3 18.0 %collect.1 = (f32[5,8,8,256]{3,2,1,0:T(8,128)S(1)}, s32[1,8192]{1,0:T(1,128)S(1)}, f32[4,2,3,8,512]{4,3,2,1,0:T(8,128)S(1)}, f32[4,2,22,8,128]{4,3,2,1,0:T(8,128)S(1)}) custom-call(s32[1,1]{1,0:T(1,128)S(6)} %copy.10.count, s32[1,8192]{1,0:T(1,128)} %bitcast.6, s32[1,8192]{1,0:T(1,128)} %cell_far.1, f32[1,8192]{1,0:T(1,128)} %volume_far.1, ...), custom_call_target="tpu_custom_call" | custom-call | tf_op jit(solution)/shard_map/collect/pallas_call | solution.py:710
  19.3 0.0 copy-start
  19.3 0.0 copy-start.1
  19.3 4.6 %deposit.1.target = f32[4,8,16,512]{3,2,1,0:T(8,128)S(1)} custom-call(f32[5,64,256]{2,1,0:T(8,128)S(1)} %bitcast.3), custom_call_target="tpu_custom_call" | custom-call | tf_op jit(solution)/shard_map/deposit/pallas_call | solution.py:753
  23.9 0.0 copy-done
  24.0 0.0 copy-done.1
  24.0 27.9 %sweeps.1.smooth = f32[4,8,16,512]{3,2,1,0:T(8,128)S(1)} custom-call(f32[8,16,512]{2,1,0:T(8,128)S(1)} %copy-done.1, f32[3,8,16,512]{3,2,1,0:T(8,128)S(1)} %copy-done, f32[4,2,3,8,512]{4,3,2,1,0:T(8,128)S(1)} %get-tuple-element.8.prior_rows, f32[4,2,22,8,128]{4,3,2,1,0:T(8,128)S(1)} %get-tuple-element.9.prior_cols, f32[4,8,16,512]{3,2,1,0:T(8,128)S(1)} %deposit.1.target), custom_call_target="tpu_custom_call" | custom-call | tf_op jit(solution)/shard_map/sweeps/pallas_call | solution.py:763
  51.9 8.3 %gather.1 = (f32[4,8,16,512]{3,2,1,0:T(8,128)}, f32[4,64,256]{2,1,0:T(8,128)S(1)}) custom-call(f32[4,8,16,512]{3,2,1,0:T(8,128)S(1)} %sweeps.1.smooth, f32[5,64,256]{2,1,0:T(8,128)S(1)} %bitcast.4), custom_call_target="tpu_custom_call" | custom-call | tf_op jit(solution)/shard_map/gather/pallas_call | solution.py:772
  60.1 11.7 %feedback.1 = f32[4,1,8192]{2,1,0:T(1,128)S(1)} custom-call(f32[4,8,8,256]{3,2,1,0:T(8,128)S(1)} %bitcast.5, s32[1,8192]{1,0:T(1,128)S(1)} %get-tuple-element.13.slots), custom_call_target="tpu_custom_call" | custom-call | tf_op jit(solution)/shard_map/feedback/pallas_call | solution.py:784
  71.8 0.7 copy.11
Async XLA Ops:
  19.3 4.7 %copy-start = (f32[3,8,16,512]{3,2,1,0:T(8,128)S(1)}, f32[3,8,16,512]{3,2,1,0:T(8,128)}, u32[]{:S(2)}) copy-start(f32[3,8,16,512]{3,2,1,0:T(8,128)} %prior.1) | copy-start | bytes 2359300
  19.3 4.7 %copy-start.1 = (f32[8,16,512]{2,1,0:T(8,128)S(1)}, f32[8,16,512]{2,1,0:T(8,128)}, u32[]{:S(2)}) copy-start(f32[8,16,512]{2,1,0:T(8,128)} %solid.1) | copy-start | bytes 786436

commit v3 on v2

--- a/solution.py
+++ b/solution.py
@@ -148,73 +148,97 @@
     out[0] = jnp.minimum(out[0], PHI_LIMIT)
 
 
-def gather_kernel(bins, smooth, ids_ref, fields, out, tables):
+def fill_table(bins, table, fields):
+    comps = len(fields)
+    for c, value in enumerate(fields):
+        high, low = two_parts(value)
+        for part in range(bins.parts):
+            lanes = slice(part * bins.cols, (part + 1) * bins.cols)
+            first = c * bins.rows + part * bins.width_x
+            table[pl.ds(first, bins.width_x)] = high[:, lanes]
+            table[pl.ds(comps * bins.rows + first, bins.width_x)] = low[:, lanes]
+
+
+def fields_of(smooth, layer, comps):
+    void = 1.0 - smooth[0, layer]
+    return [void if c == 0 else -smooth[c, layer] / void for c in comps]
+
+
+def near_values(bins, tables, ids_ref, lines, out):
+    rows, cols, half = bins.rows, bins.cols, bins.line // 2
+    height = tables.shape[1]
+    comps = height // (2 * rows)
+    for j in lines:
+        for h in range(2):
+            lanes = slice(h * half, (h + 1) * half)
+            ids = [ids_ref[0, pl.ds(o * bins.layers + j, 1), lanes] for o in range(bins.span)]
+            ids = jnp.concatenate(ids, axis=1).astype(jnp.int32) - 1
+            place, col = bins.place(ids)
+            low, high = max(j - 1 + h, 0), min(j + h, bins.layers - 1)
+            number = high - low + 1
+            table = tables[low : high + 1].reshape(number * height, cols)
+            wide = jnp.dot(table, hot_at(col, cols), preferred_element_type=F32)
+            row = lax.broadcasted_iota(jnp.int32, (rows, ids.shape[1]), 0)
+            here = [row == place - layer * rows for layer in range(low, high + 1)]
+            for c in range(comps):
+                found = 0.0
+                for k in range(number):
+                    first = k * height + c * rows
+                    second = first + comps * rows
+                    value = wide[first : first + rows] + wide[second : second + rows]
+                    found = jnp.where(here[k], value, found)
+                found = jnp.sum(found, axis=0, keepdims=True)
+                for o in range(bins.span):
+                    out(c, o, j, lanes, found[:, o * half : (o + 1) * half])
+
+
+def fields_kernel(bins, smooth, ids_ref, fields, early_tables, late_tables, out, tables):
     comps = smooth.shape[0]
-    rows, cols, width_x = bins.rows, bins.cols, bins.width_x
+    rows, cols = bins.rows, bins.cols
+    early = comps // 2
 
     def table_step(layer, carry):
-        void = 1.0 - smooth[0, layer]
+        values = fields_of(smooth, layer, range(comps))
         for c in range(comps):
-            value = void if c == 0 else -smooth[c, layer] / void
-            fields[c, layer] = value
-            high, low = two_parts(value)
-            for part in range(bins.parts):
-                lanes = slice(part * cols, (part + 1) * cols)
-                first = c * rows + part * width_x
-                tables[layer, pl.ds(first, width_x)] = high[:, lanes]
-                tables[layer, pl.ds(comps * rows + first, width_x)] = low[:, lanes]
+            fields[c, layer] = values[c]
+        fill_table(bins, early_tables.at[layer], values[:early])
+        fill_table(bins, late_tables.at[layer], values[early:])
         return carry
 
     lax.fori_loop(0, bins.layers, table_step, 0)
-
-    def found(layer, place, hot):
-        wide = jnp.dot(tables[layer], hot, preferred_element_type=F32)
-        row = lax.broadcasted_iota(jnp.int32, (rows, place.shape[1]), 0)
-        here = row == place
-        values = []
-        for c in range(comps):
-            value = wide[c * rows : (c + 1) * rows] + wide[(comps + c) * rows : (comps + c + 1) * rows]
-            values.append(jnp.sum(jnp.where(here, value, 0.0), axis=0, keepdims=True))
-        return values
-
-    if bins.binned:
-        half = bins.line // 2
-
-        for j in range(bins.layers):
-            ids = bins.flat(ids_ref, 0, j).astype(jnp.int32) - 1
-            place, col = bins.place(ids)
-            hot = hot_at(col, cols)
-            n = ids.shape[1] // 2
-            own = found(j, place - j * rows, hot)
-            low, high = max(j - 1, 0), min(j + 1, bins.layers - 1)
-            left = found(low, place[:, :n] - (j - 1) * rows, hot[:, :n])
-            right = found(high, place[:, n:] - (j + 1) * rows, hot[:, n:])
-            for c in range(comps):
-                value = own[c] + jnp.concatenate([left[c], right[c]], axis=1)
-                for at, (line, lanes) in enumerate(bins.pieces(j)):
-                    out[c, line, lanes] = value[:, at * half : (at + 1) * half]
-    else:
-        out[...] = jnp.zeros_like(out)
+    out[...] = jnp.zeros_like(out)
 
     @pl.when(bins.any_stray(ids_ref))
     def _():
+        def all_step(layer, carry):
+            fill_table(bins, tables.at[layer], [fields[c, layer] for c in range(comps)])
+            return carry
+
+        lax.fori_loop(0, bins.layers, all_step, 0)
+
         def line_step(g, carry):
             ids, mask = bins.stray_group(ids_ref, g)
             place, col = bins.place(ids)
-            place = jnp.where(mask, place, -1)
             hot = hot_at(col, cols)
+            row = lax.broadcasted_iota(jnp.int32, (rows, ids.shape[1]), 0)
 
             def layer_step(layer, total):
-                at = jnp.where(place >= 0, place - layer * rows, -1)
-                more = found(layer, at, hot)
-                return [t + m for t, m in zip(total, more)]
+                wide = jnp.dot(tables[layer], hot, preferred_element_type=F32)
+                here = (row == place - layer * rows) & mask
+                more = []
+                for c in range(comps):
+                    second = (comps + c) * rows
+                    value = wide[c * rows : (c + 1) * rows] + wide[second : second + rows]
+                    value = jnp.where(here, value, 0.0)
+                    more.append(total[c] + jnp.sum(value, axis=0, keepdims=True))
+                return more
 
             zero = [jnp.zeros(ids.shape, F32)] * comps
             total = lax.fori_loop(0, bins.layers, layer_step, zero)
+            n = bins.line
             for c in range(comps):
-                n = bins.line
                 block = [total[c][:, k * n : (k + 1) * n] for k in range(8)]
-                out[c, pl.ds(pl.multiple_of(g * 8, 8), 8), :] += jnp.concatenate(block, axis=0)
+                out[c, pl.ds(pl.multiple_of(g * 8, 8), 8), :] = jnp.concatenate(block, axis=0)
             return carry
 
         lax.fori_loop(0, bins.lines // 8, line_step, 0)
@@ -281,27 +305,38 @@
     def start(self):
         for side in range(2):
             self._when(X_STEPS[side], lambda: self.rows(side).start())
-        for side in range(2):
-            self._when(Y_STEPS[side], lambda: self.cols(0, side).start())
-
-    def forward(self):
+        self.start_cols((0,))
+
+    def start_cols(self, parts):
+        for part in parts:
+            for side in range(2):
+                self._when(Y_STEPS[side], lambda: self.cols(part, side).start())
+
+    def rows_arrive(self):
         for side in range(2):
             self._when(X_STEPS[1 - side], lambda: self.rows(side).wait_recv())
-        for part in (1, 2):
-            for side in range(2):
-                self._when(Y_STEPS[side], lambda: self.cols(part, side).start())
-
-    def arrive(self):
-        for part in range(3):
+
+    def forward(self):
+        self.rows_arrive()
+        self.start_cols((1, 2))
+
+    def arrive(self, parts=(0, 1, 2)):
+        for part in parts:
             for side in range(2):
                 self._when(Y_STEPS[1 - side], lambda: self.cols(part, side).wait_recv())
 
-    def sent(self):
+    def rows_sent(self):
         for side in range(2):
             self._when(X_STEPS[side], lambda: self.rows(side).wait_send())
-        for part in range(3):
+
+    def cols_sent(self, parts=(0, 1, 2)):
+        for part in parts:
             for side in range(2):
                 self._when(Y_STEPS[side], lambda: self.cols(part, side).wait_send())
+
+    def sent(self):
+        self.rows_sent()
+        self.cols_sent()
 
 
 HALO_COPIES = 8
@@ -327,7 +362,6 @@
     part_rows = slab.shape[1]
     width_x, width_y = solid.shape[1:]
     comps = 1 + prior.shape[0]
-    total_x = width_x + 2 * RIM
 
     barrier = pltpu.get_barrier_semaphore()
     for k in range(1, span_size):
@@ -383,20 +417,11 @@
 
         @pl.when(jnp.logical_not(grid.has(*Y_STEPS[side])))
         def _(side=side):
-            cols_in[:, side] = jnp.zeros((comps, total_x, layers, LANES), F32)
-
-    def edge(part, side):
-        if part == 0:
-            return cols_out.at[:, side]
-        lanes = pl.ds(0 if side == 0 else width_y - LANES, LANES)
-        return rows_in.at[:, part - 1, :, :, lanes]
-
-    def columns(part, side):
-        first, number = ((RIM, width_x), (0, RIM), (RIM + width_x, RIM))[part]
-        return cols_in.at[:, side, pl.ds(first, number)]
+            cols_in[:, side] = jnp.zeros((comps, width_x, layers, LANES), F32)
 
     halo = Halo(
-        grid, lambda side: rows_out.at[:, side], lambda side: rows_in.at[:, side], edge, columns,
+        grid, lambda side: rows_out.at[:, side], lambda side: rows_in.at[:, side],
+        lambda part, side: cols_out.at[:, side], lambda part, side: cols_in.at[:, side],
         lambda at: halo_send.at[at], lambda at: halo_recv.at[at],
     )
     pl.semaphore_wait(barrier, span_size - 1 + grid.around(Y_STEPS))
@@ -474,16 +499,18 @@
                 )
             )
             copies[-1].start()
-    halo.forward()
-    halo.arrive()
     for copy in copies:
         copy.wait()
-    halo.sent()
+    halo.rows_arrive()
+    halo.arrive((0,))
+    halo.rows_sent()
+    halo.cols_sent((0,))
 
 
 def sweeps_kernel(
-    solid, prior, prior_rows, prior_cols, target, out,
-    source, first, second, middle, source_cols, middle_cols, send_sem, recv_sem,
+    bins, solid, prior, prior_rows, prior_cols, target, ids_ref, out, early_values,
+    source, first, second, middle, source_cols, middle_cols, corners, tables, send_sem, recv_sem,
+    corner_send, corner_recv,
 ):
     grid = Grid()
     comps, layers, width_x, width_y = target.shape
@@ -521,6 +548,14 @@
             lambda at: send_sem.at[c, phase, at], lambda at: recv_sem.at[c, phase, at],
         )
 
+    def corner_edge(part, side):
+        lanes = pl.ds(0 if side == 0 else width_y - LANES, LANES)
+        return prior_rows.at[:, part - 1, :, :, lanes]
+
+    around = Halo(
+        grid, None, None, corner_edge, lambda part, side: corners.at[:, side, part - 1],
+        lambda at: corner_send.at[at], lambda at: corner_recv.at[at],
+    )
     halos = [[halo_of(c, phase) for phase in range(2)] for c in range(comps)]
     lane = lax.broadcasted_iota(jnp.int32, (1, layers, LANES), 2)
 
@@ -536,11 +571,12 @@
             first[c, RIM + x, :, own] = field[:, x, :]
         first[c, pl.ds(0, RIM), :, own] = prior_rows[c, 0]
         first[c, pl.ds(RIM + width_x, RIM), :, own] = prior_rows[c, 1]
-        fill_cols(first, c, prior_cols)
+        first[c, own_rows, :, rest] = jnp.where(lane < LANES // 2, prior_cols[c, 1], prior_cols[c, 0])
 
     pl.semaphore_wait(barrier, grid.around(X_STEPS + Y_STEPS))
     for c in range(comps):
         halos[c][0].start()
+    around.start_cols((1, 2))
     for side, at in ((0, 0), (1, RIM + width_x)):
 
         @pl.when(jnp.logical_not(grid.has(*X_STEPS[side])))
@@ -553,6 +589,7 @@
         def _(side=side):
             for buffer in (source_cols, middle_cols):
                 buffer[:, side] = jnp.zeros((comps, total_x, layers, LANES), F32)
+            corners[:, side] = jnp.zeros((comps, 2, RIM, layers, LANES), F32)
 
     lanes = lax.broadcasted_iota(jnp.int32, (layers, width_y + LANES), 1)
     known = lanes < width_y
@@ -605,51 +642,86 @@
             out[c, :, x, :] = relax(c, RIM + x, before, here, after)[:, :width_y]
             before, here = here, after
 
+    around.arrive((1, 2))
+    for c in range(comps):
+        for part, at in ((0, 0), (1, RIM + width_x)):
+            first[c, pl.ds(at, RIM), :, rest] = jnp.where(
+                lane < LANES // 2, corners[c, 1, part], corners[c, 0, part]
+            )
     halos[0][0].forward()
     for c in range(comps):
         if c + 1 < comps:
             halos[c + 1][0].forward()
         first_half(c)
+    early = early_values.shape[0]
+    parts = comps - early
+
+    early_values[...] = jnp.zeros_like(early_values)
+
+    def put(c, owner, line, lanes, value):
+        early_values[c, owner, pl.ds(line, 1), lanes] = value
+
     halos[0][1].forward()
     for c in range(comps):
         if c + 1 < comps:
             halos[c + 1][1].forward()
         second_half(c)
+        if not bins.binned:
+            continue
+        if c == early - 1:
+
+            def table_step(layer, carry):
+                fill_table(bins, tables.at[layer], fields_of(out, layer, range(early)))
+                return carry
+
+            lax.fori_loop(0, layers, table_step, 0)
+        if early - 1 <= c < comps - 1:
+            at = c - early + 1
+            share = layers // (2 * parts)
+            lines = range(share * at, share * (at + 1))
+            near_values(bins, tables, ids_ref, lines, put)
     for c in range(comps):
         for phase in range(2):
             halos[c][phase].sent()
-
-
-def feedback_kernel(wide, values, slots, out, table, hots, send_sem, recv_sem, own_sem):
+    around.cols_sent((1, 2))
+
+
+def feedback_kernel(
+    bins, wide, ids_ref, early_values, early_tables, late_tables, strays, slots, out,
+    values, table, hots, send_sem, recv_sem, own_sem,
+):
     grid = Grid()
     comps, span_size, per, cols = values.shape
     lines = span_size * per
     part_rows = slots.shape[1]
+    early = early_values.shape[0]
     barrier = pltpu.get_barrier_semaphore()
     for k in range(1, span_size):
         to = lax.rem(grid.span + k, span_size)
         pl.semaphore_signal(barrier, inc=1, device_id=(to, grid.depth), device_id_type=MESH)
-    def lanes_at(b):
-        return pl.ds(pl.multiple_of(b * wide, wide), wide)
-
-    def hot_step(b, carry):
-        lanes = lanes_at(b)
-        hots[:, lanes] = hot_at(lax.bitwise_and(slots[:, lanes], cols - 1), cols)
-        return carry
-
-    lax.fori_loop(0, part_rows // wide, hot_step, 0)
-    pl.semaphore_wait(barrier, span_size - 1)
-    groups = (pl.ds(0, comps // 2), pl.ds(comps // 2, comps - comps // 2))
+
+    def put(c, owner, line, lanes, value):
+        more = strays[early + c, owner, pl.ds(line, 1), lanes]
+        values[early + c, owner, pl.ds(line, 1), lanes] = value + more
+
+    def put_early(c, owner, line, lanes, value):
+        more = strays[c, owner, pl.ds(line, 1), lanes]
+        values[c, owner, pl.ds(line, 1), lanes] = value + more
+
+    values[pl.ds(0, early)] = early_values[...] + strays[pl.ds(0, early)]
     copies = []
-    for at, mine in enumerate(groups):
-        own = pltpu.make_async_copy(
-            values.at[mine, grid.span], table.at[mine, grid.span], own_sem.at[at]
-        )
-        own.start()
-        copies.append([own])
+
+    def send(first, number):
+        mine = pl.ds(first, number)
+        at = len(copies)
+        started = [
+            pltpu.make_async_copy(
+                values.at[mine, grid.span], table.at[mine, grid.span], own_sem.at[at]
+            )
+        ]
         for k in range(1, span_size):
             to = lax.rem(grid.span + k, span_size)
-            copies[at].append(
+            started.append(
                 pltpu.make_async_remote_copy(
                     src_ref=values.at[mine, to],
                     dst_ref=table.at[mine, grid.span],
@@ -659,10 +731,32 @@
                     device_id_type=MESH,
                 )
             )
-            copies[at][-1].start()
-
-    for at, mine in enumerate(groups):
-        for copy in copies[at]:
+        for copy in started:
+            copy.start()
+        copies.append((mine, started))
+
+    half = bins.layers // 2
+    if bins.binned:
+        near_values(bins, early_tables, ids_ref, range(half, bins.layers), put_early)
+    else:
+        values[pl.ds(early, comps - early)] = strays[pl.ds(early, comps - early)]
+    pl.semaphore_wait(barrier, span_size - 1)
+    send(0, early)
+    if bins.binned:
+        near_values(bins, late_tables, ids_ref, range(bins.layers), put)
+    send(early, comps - early)
+
+    def lanes_at(b):
+        return pl.ds(pl.multiple_of(b * wide, wide), wide)
+
+    def hot_step(b, carry):
+        lanes = lanes_at(b)
+        hots[:, lanes] = hot_at(lax.bitwise_and(slots[:, lanes], cols - 1), cols)
+        return carry
+
+    lax.fori_loop(0, part_rows // wide, hot_step, 0)
+    for mine, started in copies:
+        for copy in started:
             copy.wait()
         number = mine.size
         high, low = two_parts(table[mine].reshape(number * lines, cols))
@@ -715,7 +809,7 @@
             jax.ShapeDtypeStruct((5, span_size, per, cols), F32),
             jax.ShapeDtypeStruct((1, part_rows), jnp.int32),
             jax.ShapeDtypeStruct((4, 2, RIM, layers, width_y), F32),
-            jax.ShapeDtypeStruct((4, 2, total_x, layers, LANES), F32),
+            jax.ShapeDtypeStruct((4, 2, width_x, layers, LANES), F32),
         ),
         in_specs=[SMEM] + [HBM] * 6,
         out_specs=(VMEM,) * 4,
@@ -760,34 +854,46 @@
     )(recv)
     whole = pltpu.VMEM((4, total_x, layers, width_y + LANES), F32)
     columns = pltpu.VMEM((4, 2, total_x, layers, LANES), F32)
-    smooth = pl.pallas_call(
-        sweeps_kernel,
-        out_shape=jax.ShapeDtypeStruct(target.shape, F32),
-        in_specs=[VMEM] * 5,
-        out_specs=VMEM,
-        scratch_shapes=[whole] * 4 + [columns] * 2 + [dma((4, 2, HALO_COPIES))] * 2,
+    slots_of = (span_size, per, cols)
+    smooth, early_values = pl.pallas_call(
+        functools.partial(sweeps_kernel, bins),
+        out_shape=(
+            jax.ShapeDtypeStruct(target.shape, F32),
+            jax.ShapeDtypeStruct((2, *slots_of), F32),
+        ),
+        in_specs=[VMEM] * 6,
+        out_specs=(VMEM, VMEM),
+        scratch_shapes=[whole] * 4
+        + [columns] * 2
+        + [pltpu.VMEM((4, 2, 2, RIM, layers, LANES), F32)]
+        + [pltpu.VMEM((layers, 4 * bins.rows, bins.cols), BF)]
+        + [dma((4, 2, HALO_COPIES))] * 2
+        + [dma((HALO_COPIES,))] * 2,
         compiler_params=far(0),
         name="sweeps",
-    )(prior_solid, prior_drag, prior_rows, prior_cols, target)
-    fields, values = pl.pallas_call(
-        functools.partial(gather_kernel, bins),
+    )(prior_solid, prior_drag, prior_rows, prior_cols, target, recv)
+    fields, early_tables, late_tables, strays = pl.pallas_call(
+        functools.partial(fields_kernel, bins),
         out_shape=(
             jax.ShapeDtypeStruct((4, layers, width_x, width_y), F32),
+            jax.ShapeDtypeStruct((layers, 4 * bins.rows, bins.cols), BF),
+            jax.ShapeDtypeStruct((layers, 4 * bins.rows, bins.cols), BF),
             jax.ShapeDtypeStruct((4, lines, cols), F32),
         ),
         in_specs=[VMEM] * 2,
-        out_specs=(VMEM, VMEM),
+        out_specs=(VMEM,) * 4,
         scratch_shapes=[pltpu.VMEM((layers, 8 * bins.rows, bins.cols), BF)],
         compiler_params=LIMIT,
-        name="gather",
+        name="fields",
     )(smooth, recv)
     feedback = pl.pallas_call(
-        functools.partial(feedback_kernel, wide),
+        functools.partial(feedback_kernel, bins, wide),
         out_shape=jax.ShapeDtypeStruct((4, 1, part_rows), F32),
-        in_specs=[VMEM] * 2,
+        in_specs=[VMEM] * 6,
         out_specs=VMEM,
         scratch_shapes=[
-            pltpu.VMEM((4, span_size, per, cols), F32),
+            pltpu.VMEM((4, *slots_of), F32),
+            pltpu.VMEM((4, *slots_of), F32),
             pltpu.VMEM((cols, part_rows), BF),
             dma((2, span_size)),
             dma((2, span_size)),
@@ -795,7 +901,7 @@
         ],
         compiler_params=far(2),
         name="feedback",
-    )(values.reshape(4, span_size, per, cols), slots)
+    )(recv, early_values, early_tables, late_tables, strays.reshape(4, *slots_of), slots)
     return (fields, feedback)
 
 

time: 72.6 us -> 67.6 us (0.931)
  Pallas kernels: 70.5 us -> 65.4 us
    pallas_call x3, Pallas kernels: 47.8 us -> 42.8 us  [the longest x1 29.7 us: on_device(): pl.pallas_call(functools.partial(sweeps_kernel, bins), out_shape=(jax.Sha...]
where the time goes in v3:
time: 67.6 us; the launch traced here: 67.4 us
  Pallas kernels  65.4 us (97%)
  between operations  1.34 us (2%)
    pallas_call x1, Pallas kernels, on_device(): pl.pallas_call(functools.partial(sweeps_kernel, bins), out_shape=(jax.Sha...  29.7 us
    pallas_call x1, Pallas kernels, on_device(): pl.pallas_call(functools.partial(collect_kernel, cap, block, wide, layers...  18 us
    pallas_call x1, Pallas kernels, on_device(): pl.pallas_call(functools.partial(feedback_kernel, bins, wide), out_shape=...  11.7 us
    pallas_call x1, Pallas kernels, on_device(): pl.pallas_call(functools.partial(deposit_kernel, bins), out_shape=jax.Sha...  4.64 us

profile of v3, /device:TPU:1, one launch (start us, length us, event | category | flops | bytes accessed | tf_op | source)
XLA Modules:
  0.0 67.4 jit_solution(4094688337499748736)
XLA Ops:
  1.3 18.0 %collect.1 = (f32[5,8,8,256]{3,2,1,0:T(8,128)S(1)}, s32[1,8192]{1,0:T(1,128)S(1)}, f32[4,2,3,8,512]{4,3,2,1,0:T(8,128)S(1)}, f32[4,2,16,8,128]{4,3,2,1,0:T(8,128)S(1)}) custom-call(s32[1,1]{1,0:T(1,128)S(6)} %copy.10.count, s32[1,8192]{1,0:T(1,128)} %bitcast.8, s32[1,8192]{1,0:T(1,128)} %cell_far.1, f32[1,8192]{1,0:T(1,128)} %volume_far.1, ...), custom_call_target="tpu_custom_call" | custom-call | tf_op jit(solution)/shard_map/collect/pallas_call | solution.py:804
  19.3 0.0 copy-start
  19.3 0.0 copy-start.1
  19.3 4.6 %deposit.1.target = f32[4,8,16,512]{3,2,1,0:T(8,128)S(1)} custom-call(f32[5,64,256]{2,1,0:T(8,128)S(1)} %bitcast.3), custom_call_target="tpu_custom_call" | custom-call | tf_op jit(solution)/shard_map/deposit/pallas_call | solution.py:847
  23.9 0.0 copy-done
  23.9 0.0 copy-done.1
  24.0 29.7 %sweeps.1 = (f32[4,8,16,512]{3,2,1,0:T(8,128)S(1)}, f32[2,8,8,256]{3,2,1,0:T(8,128)S(1)}) custom-call(f32[8,16,512]{2,1,0:T(8,128)S(1)} %copy-done.1, f32[3,8,16,512]{3,2,1,0:T(8,128)S(1)} %copy-done, f32[4,2,3,8,512]{4,3,2,1,0:T(8,128)S(1)} %get-tuple-element.12.prior_rows, f32[4,2,16,8,128]{4,3,2,1,0:T(8,128)S(1)} %get-tuple-element.13.prior_cols, ...), custom_call_target="tpu_custom_call" | custom-call | tf_op jit(solution)/shard_map/sweeps/pallas_call | solution.py:858
  53.7 1.4 %fields.1 = (f32[4,8,16,512]{3,2,1,0:T(8,128)}, bf16[8,128,256]{2,1,0:T(8,128)(2,1)S(1)}, bf16[8,128,256]{2,1,0:T(8,128)(2,1)S(1)}, f32[4,64,256]{2,1,0:T(8,128)S(1)}) custom-call(f32[4,8,16,512]{3,2,1,0:T(8,128)S(1)} %get-tuple-element.15.smooth, f32[5,64,256]{2,1,0:T(8,128)S(1)} %bitcast.5), custom_call_target="tpu_custom_call" | custom-call | tf_op jit(solution)/shard_map/fields/pallas_call | solution.py:875
  55.0 11.7 %feedback.1 = f32[4,1,8192]{2,1,0:T(1,128)S(1)} custom-call(f32[5,64,256]{2,1,0:T(8,128)S(1)} %bitcast.6, f32[2,8,8,256]{3,2,1,0:T(8,128)S(1)} %get-tuple-element.17.early_values, bf16[8,128,256]{2,1,0:T(8,128)(2,1)S(1)} %get-tuple-element.18.early_tables, bf16[8,128,256]{2,1,0:T(8,128)(2,1)S(1)} %get-tuple-element.19.late_tables, ...), custom_call_target="tpu_custom_call" | custom-call | tf_op jit(solution)/shard_map/feedback/pallas_call | solution.py:889
  66.7 0.7 copy.11
Async XLA Ops:
  19.3 4.7 %copy-start = (f32[3,8,16,512]{3,2,1,0:T(8,128)S(1)}, f32[3,8,16,512]{3,2,1,0:T(8,128)}, u32[]{:S(2)}) copy-start(f32[3,8,16,512]{3,2,1,0:T(8,128)} %prior.1) | copy-start | bytes 2359300
  19.3 4.7 %copy-start.1 = (f32[8,16,512]{2,1,0:T(8,128)S(1)}, f32[8,16,512]{2,1,0:T(8,128)}, u32[]{:S(2)}) copy-start(f32[8,16,512]{2,1,0:T(8,128)} %solid.1) | copy-start | bytes 786436

commit v4 on v3

--- a/solution.py
+++ b/solution.py
@@ -73,17 +73,6 @@
         mask = self.strays(ids, line, lane)
         return jnp.max(jnp.where(mask, 1.0, 0.0)) > 0.0
 
-    def pieces(self, j):
-        half = self.line // 2
-        return [
-            (pl.ds(o * self.layers + j, 1), slice(h * half, (h + 1) * half))
-            for h in range(2)
-            for o in range(self.span)
-        ]
-
-    def flat(self, ref, c, j):
-        return jnp.concatenate([ref[c, line, lanes] for line, lanes in self.pieces(j)], axis=1)
-
     def group(self, ref, c, g):
         block = ref[c, pl.ds(pl.multiple_of(g * 8, 8), 8), :]
         return jnp.concatenate([block[k : k + 1] for k in range(8)], axis=1)
@@ -96,39 +85,46 @@
         return ids, self.strays(ids, line, lax.bitwise_and(lane, self.line - 1))
 
 
-def deposit_kernel(bins, recv, out):
-    comps = out.shape[0]
-    rows, cols, width_x = bins.rows, bins.cols, bins.width_x
-    out[...] = jnp.zeros_like(out)
-
-    def add(layer, sums):
-        for c in range(comps):
-            for part in range(bins.parts):
-                lanes = slice(part * cols, (part + 1) * cols)
-                first = c * rows + part * width_x
-                out[c, layer, :, lanes] += sums[first : first + width_x]
-
-    if bins.binned:
-
-        for j in range(bins.layers):
-            flat = [bins.flat(recv, c, j) for c in range(comps + 1)]
-            ids = flat[0].astype(jnp.int32) - 1
-            place, col = bins.place(ids)
-            hot = hot_at(col, cols)
-            parts = [two_parts(v) for v in flat[1:]]
-            n = ids.shape[1] // 2
-
-            def sums(layer, lanes, place=place, parts=parts, hot=hot):
-                mask = hot_at(place[:, lanes] - layer * rows, rows)
-                left = [mask * p[k][:, lanes] for k in range(2) for p in parts]
-                both = nt_dot(jnp.concatenate(left, axis=0), hot[:, lanes])
-                return both[: comps * rows] + both[comps * rows :]
-
-            add(j, sums(j, slice(0, 2 * n)))
-            if j > 0:
-                add(j - 1, sums(j - 1, slice(0, n)))
-            if j < bins.layers - 1:
-                add(j + 1, sums(j + 1, slice(n, 2 * n)))
+def add_sums(bins, out, layer, sums):
+    for c in range(out.shape[0]):
+        for part in range(bins.parts):
+            lanes = slice(part * bins.cols, (part + 1) * bins.cols)
+            first = c * bins.rows + part * bins.width_x
+            out[c, layer, :, lanes] += sums[first : first + bins.width_x]
+
+
+def near_sums(bins, recv, owners, out):
+    comps, half, rows = out.shape[0], bins.line // 2, bins.rows
+    for j in range(bins.layers):
+
+        def flat(c, j=j):
+            pieces = [
+                recv[c, o, pl.ds(j, 1), h * half : (h + 1) * half] for h in range(2) for o in owners
+            ]
+            return jnp.concatenate(pieces, axis=1)
+
+        ids = flat(0).astype(jnp.int32) - 1
+        place, col = bins.place(ids)
+        hot = hot_at(col, bins.cols)
+        parts = [two_parts(flat(1 + c)) for c in range(comps)]
+        n = ids.shape[1] // 2
+
+        def sums(layer, lanes, place=place, hot=hot, parts=parts):
+            mask = hot_at(place[:, lanes] - layer * rows, rows)
+            left = [mask * p[k][:, lanes] for k in range(2) for p in parts]
+            both = nt_dot(jnp.concatenate(left, axis=0), hot[:, lanes])
+            add_sums(bins, out, layer, both[: comps * rows] + both[comps * rows :])
+
+        sums(j, slice(0, 2 * n))
+        if j > 0:
+            sums(j - 1, slice(0, n))
+        if j < bins.layers - 1:
+            sums(j + 1, slice(n, 2 * n))
+
+
+def deposit_kernel(bins, near, recv, out):
+    comps, rows, cols = out.shape[0], bins.rows, bins.cols
+    out[...] = near[...]
 
     @pl.when(bins.any_stray(recv))
     def _():
@@ -138,7 +134,7 @@
             values = [jnp.where(mask, bins.group(recv, 1 + c, g), 0.0) for c in range(comps)]
 
             def layer_step(layer, inner):
-                add(layer, spread(values, place - layer * rows, col, rows, cols))
+                add_sums(bins, out, layer, spread(values, place - layer * rows, col, rows, cols))
                 return inner
 
             return lax.fori_loop(0, bins.layers, layer_step, carry)
@@ -247,6 +243,7 @@
 MESH = pl.DeviceIdType.MESH
 RIM = SWEEPS // 2
 LANES = 128
+BATCH = 2
 
 
 class Grid:
@@ -343,8 +340,8 @@
 
 
 def collect_kernel(
-    cap, block, wide, layers, shift, count, slab_far, cell_far, volume_far, drag_far, solid_far,
-    prior_far, recv, slots, rows_in, cols_in, packed, rows_out, cols_out,
+    bins, cap, block, wide, layers, shift, count, slab_far, cell_far, volume_far, drag_far, solid_far,
+    prior_far, recv, slots, rows_in, cols_in, near_target, packed, rows_out, cols_out,
     slab, cell, volume, drag, solid, prior, halo_send, halo_recv, send_sem, recv_sem, own_sem,
     near_sem,
 ):
@@ -419,13 +416,21 @@
         def _(side=side):
             cols_in[:, side] = jnp.zeros((comps, width_x, layers, LANES), F32)
 
-    halo = Halo(
-        grid, lambda side: rows_out.at[:, side], lambda side: rows_in.at[:, side],
-        lambda part, side: cols_out.at[:, side], lambda part, side: cols_in.at[:, side],
-        lambda at: halo_send.at[at], lambda at: halo_recv.at[at],
-    )
+    def halo_of(at):
+        mine = pl.ds(*((0, comps // 2), (comps // 2, comps - comps // 2))[at])
+        return Halo(
+            grid,
+            lambda side: rows_out.at[mine, side],
+            lambda side: rows_in.at[mine, side],
+            lambda part, side: cols_out.at[mine, side],
+            lambda part, side: cols_in.at[mine, side],
+            lambda copy: halo_send.at[at, copy],
+            lambda copy: halo_recv.at[at, copy],
+        )
+
+    halos = [halo_of(at) for at in range(2)]
     pl.semaphore_wait(barrier, span_size - 1 + grid.around(Y_STEPS))
-    halo.start()
+    halos[0].start()
 
     before_lane = lax.broadcasted_iota(jnp.int32, (block, block), 0)
     this_lane = lax.broadcasted_iota(jnp.int32, (block, block), 1)
@@ -460,7 +465,25 @@
     near[4].wait()
     near[5].wait()
     groups = ((0, 2), (2, values - 2))
-    copies = []
+
+    def own_copy(at):
+        mine = pl.ds(*groups[at])
+        return pltpu.make_async_copy(
+            packed.at[mine, grid.span], recv.at[mine, grid.span], own_sem.at[at]
+        )
+
+    def copy_to(at, k):
+        mine = pl.ds(*groups[at])
+        to = lax.rem(grid.span + k, span_size)
+        return pltpu.make_async_remote_copy(
+            src_ref=packed.at[mine, to],
+            dst_ref=recv.at[mine, grid.span],
+            send_sem=send_sem.at[at, k],
+            recv_sem=recv_sem.at[at, k],
+            device_id=(to, grid.depth),
+            device_id_type=MESH,
+        )
+
     for at, (first_value, number) in enumerate(groups):
         mine = pl.ds(first_value, number)
 
@@ -481,39 +504,58 @@
 
         packed[mine] = jnp.zeros((number, span_size, per, cols), F32)
         lax.fori_loop(0, part_rows // wide, place_values, 0)
-        own = pltpu.make_async_copy(
-            packed.at[mine, grid.span], recv.at[mine, grid.span], own_sem.at[at]
-        )
-        own.start()
-        copies.append(own)
+        own_copy(at).start()
         for k in range(1, span_size):
-            to = lax.rem(grid.span + k, span_size)
-            copies.append(
-                pltpu.make_async_remote_copy(
-                    src_ref=packed.at[mine, to],
-                    dst_ref=recv.at[mine, grid.span],
-                    send_sem=send_sem.at[at, k],
-                    recv_sem=recv_sem.at[at, k],
-                    device_id=(to, grid.depth),
-                    device_id_type=MESH,
-                )
-            )
-            copies[-1].start()
-    for copy in copies:
-        copy.wait()
-    halo.rows_arrive()
-    halo.arrive((0,))
-    halo.rows_sent()
-    halo.cols_sent((0,))
+            copy_to(at, k).start()
+    halos[1].start()
+    near_target[...] = jnp.zeros_like(near_target)
+    for at in range(len(groups)):
+        own_copy(at).wait()
+    if bins.binned:
+        batch = math.gcd(span_size, BATCH)
+
+        def batch_step(b, carry):
+            owners = []
+            for i in range(batch):
+                k = b * batch + i
+
+                @pl.when(k > 0)
+                def _(k=k):
+                    for at in range(len(groups)):
+                        copy_to(at, k).wait_recv()
+
+                owners.append(lax.rem(grid.span + span_size - k, span_size))
+            near_sums(bins, recv, owners, near_target)
+            return carry
+
+        lax.fori_loop(0, span_size // batch, batch_step, 0)
+    else:
+        for at in range(len(groups)):
+            for k in range(1, span_size):
+                copy_to(at, k).wait_recv()
+    for at in range(len(groups)):
+        for k in range(1, span_size):
+            copy_to(at, k).wait_send()
+    for halo in halos:
+        halo.rows_arrive()
+        halo.arrive((0,))
+        halo.rows_sent()
+        halo.cols_sent((0,))
 
 
 def sweeps_kernel(
-    bins, solid, prior, prior_rows, prior_cols, target, ids_ref, out, early_values,
-    source, first, second, middle, source_cols, middle_cols, corners, tables, send_sem, recv_sem,
+    bins, solid_far, prior_far, prior_rows, prior_cols, target, ids_ref, out, early_values,
+    solid, prior, near_sem, source, first, second, middle, source_cols, middle_cols, corners, tables, send_sem, recv_sem,
     corner_send, corner_recv,
 ):
     grid = Grid()
     comps, layers, width_x, width_y = target.shape
+    near = [
+        pltpu.make_async_copy(a, b, near_sem.at[k])
+        for k, (a, b) in enumerate(((solid_far, solid), (prior_far, prior)))
+    ]
+    for copy in near:
+        copy.start()
     total_x = width_x + 2 * RIM
     own = pl.ds(0, width_y)
     rest = pl.ds(width_y, LANES)
@@ -565,6 +607,8 @@
     for c in range(comps):
         for x in range(width_x):
             source[c, RIM + x, :, own] = target[c, :, x, :]
+    for copy in near:
+        copy.wait()
     for c in range(comps):
         field = solid if c == 0 else prior.at[c - 1]
         for x in range(width_x):
@@ -801,18 +845,20 @@
     wide = math.gcd(part_rows, 2048)
     total_x = width_x + 2 * RIM
     dma = pltpu.SemaphoreType.DMA
-    recv, slots, prior_rows, prior_cols = pl.pallas_call(
+    bins = Bins(layers, width_x, width_y, span_size, lines, cols)
+    recv, slots, prior_rows, prior_cols, near_target = pl.pallas_call(
         functools.partial(
-            collect_kernel, cap, block, wide, layers, int(math.log2(width_x * width_y))
+            collect_kernel, bins, cap, block, wide, layers, int(math.log2(width_x * width_y))
         ),
         out_shape=(
             jax.ShapeDtypeStruct((5, span_size, per, cols), F32),
             jax.ShapeDtypeStruct((1, part_rows), jnp.int32),
             jax.ShapeDtypeStruct((4, 2, RIM, layers, width_y), F32),
             jax.ShapeDtypeStruct((4, 2, width_x, layers, LANES), F32),
+            jax.ShapeDtypeStruct((4, layers, width_x, width_y), F32),
         ),
         in_specs=[SMEM] + [HBM] * 6,
-        out_specs=(VMEM,) * 4,
+        out_specs=(VMEM,) * 5,
         scratch_shapes=[
             pltpu.VMEM((5, span_size, per, cols), F32),
             pltpu.VMEM((4, 2, RIM, layers, width_y), F32),
@@ -823,8 +869,8 @@
             pltpu.VMEM(part_drag.shape, F32),
             pltpu.VMEM(prior_solid.shape, F32),
             pltpu.VMEM(prior_drag.shape, F32),
-            dma((HALO_COPIES,)),
-            dma((HALO_COPIES,)),
+            dma((2, HALO_COPIES)),
+            dma((2, HALO_COPIES)),
             dma((2, span_size)),
             dma((2, span_size)),
             dma((2,)),
@@ -843,15 +889,14 @@
         ],
     )
     recv = recv.reshape(5, lines, cols)
-    bins = Bins(layers, width_x, width_y, span_size, lines, cols)
     target = pl.pallas_call(
         functools.partial(deposit_kernel, bins),
         out_shape=jax.ShapeDtypeStruct((4, layers, width_x, width_y), F32),
-        in_specs=[VMEM],
+        in_specs=[VMEM] * 2,
         out_specs=VMEM,
         compiler_params=LIMIT,
         name="deposit",
-    )(recv)
+    )(near_target, recv)
     whole = pltpu.VMEM((4, total_x, layers, width_y + LANES), F32)
     columns = pltpu.VMEM((4, 2, total_x, layers, LANES), F32)
     slots_of = (span_size, per, cols)
@@ -861,9 +906,14 @@
             jax.ShapeDtypeStruct(target.shape, F32),
             jax.ShapeDtypeStruct((2, *slots_of), F32),
         ),
-        in_specs=[VMEM] * 6,
+        in_specs=[HBM] * 2 + [VMEM] * 4,
         out_specs=(VMEM, VMEM),
-        scratch_shapes=[whole] * 4
+        scratch_shapes=[
+            pltpu.VMEM(prior_solid.shape, F32),
+            pltpu.VMEM(prior_drag.shape, F32),
+            dma((2,)),
+        ]
+        + [whole] * 4
         + [columns] * 2
         + [pltpu.VMEM((4, 2, 2, RIM, layers, LANES), F32)]
         + [pltpu.VMEM((layers, 4 * bins.rows, bins.cols), BF)]
@@ -871,7 +921,11 @@
         + [dma((HALO_COPIES,))] * 2,
         compiler_params=far(0),
         name="sweeps",
-    )(prior_solid, prior_drag, prior_rows, prior_cols, target, recv)
+    )(
+        pltpu.with_memory_space_constraint(prior_solid, pltpu.HBM),
+        pltpu.with_memory_space_constraint(prior_drag, pltpu.HBM),
+        prior_rows, prior_cols, target, recv,
+    )
     fields, early_tables, late_tables, strays = pl.pallas_call(
         functools.partial(fields_kernel, bins),
         out_shape=(

time: 67.6 us -> 66.7 us (0.987)
  Pallas kernels: 65.4 us -> 64.5 us
    pallas_call x1, Pallas kernels: 4.64 us -> 0.25 us  [on_device(): pl.pallas_call(functools.partial(deposit_kernel, bins), out_shape=jax.Sha...]
    pallas_call x1, Pallas kernels: 18 us -> 20.7 us  [on_device(): pl.pallas_call(functools.partial(collect_kernel, bins, cap, block, wide,...]
where the time goes in v4:
time: 66.7 us; the launch traced here: 66.5 us
  Pallas kernels  64.5 us (97%)
  between operations  1.31 us (2%)
    pallas_call x1, Pallas kernels, on_device(): pl.pallas_call(functools.partial(sweeps_kernel, bins), out_shape=(jax.Sha...  29.9 us
    pallas_call x1, Pallas kernels, on_device(): pl.pallas_call(functools.partial(collect_kernel, bins, cap, block, wide,...  20.7 us
    pallas_call x1, Pallas kernels, on_device(): pl.pallas_call(functools.partial(feedback_kernel, bins, wide), out_shape=...  12.1 us
    pallas_call x1, Pallas kernels, on_device(): pl.pallas_call(functools.partial(fields_kernel, bins), out_shape=(jax.Sha...  1.53 us

profile of v4, /device:TPU:1, one launch (start us, length us, event | category | flops | bytes accessed | tf_op | source)
XLA Modules:
  0.0 66.5 jit_solution(6756130402538148360)
XLA Ops:
  1.3 20.7 %collect.1 = (f32[5,8,8,256]{3,2,1,0:T(8,128)S(1)}, s32[1,8192]{1,0:T(1,128)S(1)}, f32[4,2,3,8,512]{4,3,2,1,0:T(8,128)S(1)}, f32[4,2,16,8,128]{4,3,2,1,0:T(8,128)S(1)}, f32[4,8,16,512]{3,2,1,0:T(8,128)S(1)}) custom-call(s32[1,1]{1,0:T(1,128)S(6)} %copy.10.count, s32[1,8192]{1,0:T(1,128)} %bitcast.8, s32[1,8192]{1,0:T(1,128)} %cell_far.1, ...), custom_call_target="tpu_custom_call" | custom-call | tf_op jit(solution)/shard_map/collect/pallas_call | solution.py:849
  22.0 0.2 deposit.1.target
  22.3 29.9 %sweeps.1 = (f32[4,8,16,512]{3,2,1,0:T(8,128)S(1)}, f32[2,8,8,256]{3,2,1,0:T(8,128)S(1)}) custom-call(f32[8,16,512]{2,1,0:T(8,128)} %solid_far.3, f32[3,8,16,512]{3,2,1,0:T(8,128)} %prior_far.3, f32[4,2,3,8,512]{4,3,2,1,0:T(8,128)S(1)} %get-tuple-element.13.prior_rows, f32[4,2,16,8,128]{4,3,2,1,0:T(8,128)S(1)} %get-tuple-element.14.prior_cols, ...), custom_call_target="tpu_custom_call" | custom-call | tf_op jit(solution)/shard_map/sweeps/pallas_call | solution.py:903
  52.2 1.5 %fields.1 = (f32[4,8,16,512]{3,2,1,0:T(8,128)}, bf16[8,128,256]{2,1,0:T(8,128)(2,1)S(1)}, bf16[8,128,256]{2,1,0:T(8,128)(2,1)S(1)}, f32[4,64,256]{2,1,0:T(8,128)S(1)}) custom-call(f32[4,8,16,512]{3,2,1,0:T(8,128)S(1)} %get-tuple-element.17.smooth, f32[5,64,256]{2,1,0:T(8,128)S(1)} %bitcast.5), custom_call_target="tpu_custom_call" | custom-call | tf_op jit(solution)/shard_map/fields/pallas_call | solution.py:929
  53.8 12.1 %feedback.1 = f32[4,1,8192]{2,1,0:T(1,128)S(1)} custom-call(f32[5,64,256]{2,1,0:T(8,128)S(1)} %bitcast.6, f32[2,8,8,256]{3,2,1,0:T(8,128)S(1)} %get-tuple-element.19.early_values, bf16[8,128,256]{2,1,0:T(8,128)(2,1)S(1)} %get-tuple-element.20.early_tables, bf16[8,128,256]{2,1,0:T(8,128)(2,1)S(1)} %get-tuple-element.21.late_tables, ...), custom_call_target="tpu_custom_call" | custom-call | tf_op jit(solution)/shard_map/feedback/pallas_call | solution.py:943
  65.8 0.7 copy.11

commit v5 on v4

--- a/solution.py
+++ b/solution.py
@@ -696,6 +696,8 @@
     for c in range(comps):
         if c + 1 < comps:
             halos[c + 1][0].forward()
+        else:
+            halos[0][1].forward()
         first_half(c)
     early = early_values.shape[0]
     parts = comps - early
@@ -705,7 +707,6 @@
     def put(c, owner, line, lanes, value):
         early_values[c, owner, pl.ds(line, 1), lanes] = value
 
-    halos[0][1].forward()
     for c in range(comps):
         if c + 1 < comps:
             halos[c + 1][1].forward()

time: 66.7 us -> 65.7 us (0.985)
  Pallas kernels: 64.5 us -> 63.5 us
    pallas_call x1, Pallas kernels: 29.9 us -> 28.7 us  [on_device(): pl.pallas_call(functools.partial(sweeps_kernel, bins), out_shape=(jax.Sha...]
where the time goes in v5:
time: 65.7 us; the launch traced here: 65.5 us
  Pallas kernels  63.5 us (97%)
  between operations  1.31 us (2%)
  local copies, waits for them, and re-layouts  0.66 us (1%)
    pallas_call x1, Pallas kernels, on_device(): pl.pallas_call(functools.partial(sweeps_kernel, bins), out_shape=(jax.Sha...  28.7 us
    pallas_call x1, Pallas kernels, on_device(): pl.pallas_call(functools.partial(collect_kernel, bins, cap, block, wide,...  20.7 us
    pallas_call x1, Pallas kernels, on_device(): pl.pallas_call(functools.partial(feedback_kernel, bins, wide), out_shape=...  12.3 us
    pallas_call x1, Pallas kernels, on_device(): pl.pallas_call(functools.partial(fields_kernel, bins), out_shape=(jax.Sha...  1.53 us

profile of v5, /device:TPU:1, one launch (start us, length us, event | category | flops | bytes accessed | tf_op | source)
XLA Modules:
  0.0 65.5 jit_solution(16673914985909837452)
XLA Ops:
  1.3 20.7 %collect.1 = (f32[5,8,8,256]{3,2,1,0:T(8,128)S(1)}, s32[1,8192]{1,0:T(1,128)S(1)}, f32[4,2,3,8,512]{4,3,2,1,0:T(8,128)S(1)}, f32[4,2,16,8,128]{4,3,2,1,0:T(8,128)S(1)}, f32[4,8,16,512]{3,2,1,0:T(8,128)S(1)}) custom-call(s32[1,1]{1,0:T(1,128)S(6)} %copy.10.count, s32[1,8192]{1,0:T(1,128)} %bitcast.8, s32[1,8192]{1,0:T(1,128)} %cell_far.1, ...), custom_call_target="tpu_custom_call" | custom-call | tf_op jit(solution)/shard_map/collect/pallas_call | solution.py:850
  22.0 0.2 deposit.1.target
  22.3 28.7 %sweeps.1 = (f32[4,8,16,512]{3,2,1,0:T(8,128)S(1)}, f32[2,8,8,256]{3,2,1,0:T(8,128)S(1)}) custom-call(f32[8,16,512]{2,1,0:T(8,128)} %solid_far.3, f32[3,8,16,512]{3,2,1,0:T(8,128)} %prior_far.3, f32[4,2,3,8,512]{4,3,2,1,0:T(8,128)S(1)} %get-tuple-element.13.prior_rows, f32[4,2,16,8,128]{4,3,2,1,0:T(8,128)S(1)} %get-tuple-element.14.prior_cols, ...), custom_call_target="tpu_custom_call" | custom-call | tf_op jit(solution)/shard_map/sweeps/pallas_call | solution.py:904
  51.0 1.5 %fields.1 = (f32[4,8,16,512]{3,2,1,0:T(8,128)}, bf16[8,128,256]{2,1,0:T(8,128)(2,1)S(1)}, bf16[8,128,256]{2,1,0:T(8,128)(2,1)S(1)}, f32[4,64,256]{2,1,0:T(8,128)S(1)}) custom-call(f32[4,8,16,512]{3,2,1,0:T(8,128)S(1)} %get-tuple-element.17.smooth, f32[5,64,256]{2,1,0:T(8,128)S(1)} %bitcast.5), custom_call_target="tpu_custom_call" | custom-call | tf_op jit(solution)/shard_map/fields/pallas_call | solution.py:930
  52.6 12.3 %feedback.1 = f32[4,1,8192]{2,1,0:T(1,128)S(1)} custom-call(f32[5,64,256]{2,1,0:T(8,128)S(1)} %bitcast.6, f32[2,8,8,256]{3,2,1,0:T(8,128)S(1)} %get-tuple-element.19.early_values, bf16[8,128,256]{2,1,0:T(8,128)(2,1)S(1)} %get-tuple-element.20.early_tables, bf16[8,128,256]{2,1,0:T(8,128)(2,1)S(1)} %get-tuple-element.21.late_tables, ...), custom_call_target="tpu_custom_call" | custom-call | tf_op jit(solution)/shard_map/feedback/pallas_call | solution.py:944
  64.8 0.7 %copy.11 = f32[4,1,8192]{2,1,0:T(1,128)} copy(f32[4,1,8192]{2,1,0:T(1,128)S(1)} %feedback.1) | data formatting | bytes 262144
